TPU v7x, 512 devices: a whole 4x4x16 slice. The times are simulated.
512 devices in a mesh: group: 16 (over y, x_lo, core), tile: 32 (over x_hi, z).
Axes of the slice: x: 4 (x_hi: 2, x_lo: 2; x = x_hi * 2 + x_lo), y: 4, z: 16, core: 2. Of those that a mesh axis runs over, the one named last changes fastest.
Arguments:
- checkpoint: float32 [16, 8192, 768], P(None, ('group', 'tile')), may hold values from -6 to 6
- adjoint_in: float32 [16, 8192, 768], P(None, ('group', 'tile')), may hold values from -6 to 6
- courant_x: float32 [16, 8192, 768], P(None, ('group', 'tile')), may hold values from 0.05 to 0.5
- courant_y: float32 [16, 8192, 768], P(None, ('group', 'tile')), may hold values from 0.05 to 0.5
- mixing: float32 [15, 8192, 768], P(None, ('group', 'tile')), may hold values from 0.02 to 0.3
- snd_column: int32 [512, 32, 128], P(('group', 'tile')), may hold values from 0 to 12287
- snd_count: int32 [512, 32], P(('group', 'tile')), may hold values from 32 to 128, as said below
- snd_step: int32 [512, 32, 128], P(('group', 'tile')), may hold values from 0 to 1
- snd_value: float32 [512, 32, 128], P(('group', 'tile')), may hold values from -6 to 6
- snd_weight: float32 [512, 32, 128], P(('group', 'tile')), may hold values from 0.3 to 3
- snd_kernel: float32 [512, 32, 16, 128], P(('group', 'tile')), may hold values from 0 to 0.5
Outputs:
- adjoint_out: float32 [16, 8192, 768], P(None, ('group', 'tile'))
Inputs may be any that keep to these rules, and one draw needn't show every extreme that they name: `snd_count`: at most 128; in every draw some destination tile receives 128 soundings from every source device of each group, and every source device fills all slots of some destination tile.
All inputs are finite; a program needn't handle non-finite values.
Results may differ from a plain program's by a relative error of at most 0.0001.
Values sent between devices are 32-bit elements; how exact they have to be, the bound alone decides.
No kernel may reach another device: no remote copies, remote signals or barrier semaphores. Data moves between devices by JAX's collectives and lax.ppermute only.
A program may use at most 64 MiB of HBM per device.

v0:
```python
import jax
import jax.numpy as jnp
from jax import lax
from jax.sharding import PartitionSpec as P

STEPS = 2


def padded_2(x, sides, width):
    edges = {}
    for axis, dim in sides:
        count, length = (lax.axis_size(axis), x.shape[dim])
        up = [(i, (i + 1) % count) for i in range(count)]
        last = lax.slice_in_dim(x, length - width, length, axis=dim)
        initial = lax.slice_in_dim(x, 0, width, axis=dim)
        edges[dim] = (
            lax.ppermute(last, axis, up),
            lax.ppermute(initial, axis, [(b, a) for a, b in up]),
        )
    done = []
    for _, dim in sides:
        low, high = edges[dim]
        around = [(width, width) if d in done else (0, 0) for d in range(x.ndim)]
        x = jnp.concatenate([jnp.pad(low, around), x, jnp.pad(high, around)], axis=dim)
        done.append(dim)
    return x


def from_behind(block, axis, distance):
    devices = range(lax.axis_size(axis))
    route = [((i - distance) % len(devices), i) for i in devices]
    return lax.ppermute(block, axis, route)


def in_one_piece(arrays, axis, split_dim, concat_dim, along):
    columns = [a.reshape(*a.shape[:along], -1) for a in arrays]
    both = jnp.concatenate(columns, axis=along)
    whole, at, gathered = (
        lax.all_to_all(both, axis, split_axis=split_dim, concat_axis=concat_dim, tiled=True),
        0,
        [],
    )
    for a, column in zip(arrays, columns):
        piece = whole[..., at : at + column.shape[along]]
        gathered.append(piece.reshape(*piece.shape[:along], *a.shape[along:]))
        at += column.shape[along]
    return tuple(gathered)


def sent_together(arrays, axis, split_dim, concat_dim, along):
    both = jnp.concatenate(arrays, axis=along)
    whole, at, gathered = (
        lax.all_to_all(both, axis, split_axis=split_dim, concat_axis=concat_dim, tiled=True),
        0,
        [],
    )
    for a in arrays:
        gathered.append(lax.slice_in_dim(whole, at, at + a.shape[along], axis=along))
        at += a.shape[along]
    return tuple(gathered)


def with_halo(block, sides, width):
    for axis, dim in sides:
        count = lax.axis_size(axis)
        forward = [(i, i + 1) for i in range(count - 1)]
        forward.append((count - 1, 0))
        backward = [(target, source) for source, target in forward]
        low = lax.ppermute(
            lax.slice_in_dim(block, block.shape[dim] - width, None, axis=dim), axis, forward
        )
        high = lax.ppermute(lax.slice_in_dim(block, 0, width, axis=dim), axis, backward)
        block = jnp.concatenate([low, block, high], axis=dim)
    return block


def pad_periodic(field, width, along):
    total = field.shape[along]
    return jnp.concatenate(
        [
            lax.slice_in_dim(field, total - width, total, axis=along),
            field,
            lax.slice_in_dim(field, 0, width, axis=along),
        ],
        axis=along,
    )


def sweep_forward(padded, courant_pad, along):
    interior = padded.shape[along] - 4

    def piece_of(first, last):
        return lax.slice_in_dim(padded, first, last, axis=along)

    courant_face = lax.slice_in_dim(courant_pad, 0, interior + 1, axis=along)
    fluxes = (
        courant_face
        * (
            2.0 * piece_of(2, interior + 3)
            + 5.0 * piece_of(1, interior + 2)
            - piece_of(0, interior + 1)
        )
        / 6.0
    )
    return (
        piece_of(2, interior + 2)
        + lax.slice_in_dim(fluxes, 0, interior, axis=along)
        - lax.slice_in_dim(fluxes, 1, interior + 1, axis=along)
    )


def sweep_adjoint(padded, courant_pad, along):
    interior = padded.shape[along] - 4

    def piece_of(first, last):
        return lax.slice_in_dim(padded, first, last, axis=along)

    differences = piece_of(2, interior + 4) - piece_of(1, interior + 3)
    scaled = courant_pad * differences
    return (
        piece_of(2, interior + 2)
        + (
            2.0 * lax.slice_in_dim(scaled, 0, interior, axis=along)
            + 5.0 * lax.slice_in_dim(scaled, 1, interior + 1, axis=along)
            - lax.slice_in_dim(scaled, 2, interior + 2, axis=along)
        )
        / 6.0
    )


def vertical_mix(field, mixing):
    fluxes = mixing * (field[1:] - field[:-1])
    zero_row = jnp.zeros_like(field[:1])
    return (
        field
        + jnp.concatenate([fluxes, zero_row], axis=0)
        - jnp.concatenate([zero_row, fluxes], axis=0)
    )


def horizontal(rimmed, wind_x, wind_y):
    swept = sweep_forward(rimmed, wind_x, 1)
    return sweep_forward(pad_periodic(swept, 2, 2), wind_y, 2)


def on_device(
    checkpoint,
    adjoint_in,
    courant_x,
    courant_y,
    mixing,
    snd_column,
    snd_count,
    snd_step,
    snd_value,
    snd_weight,
    snd_kernel,
):
    levels, width_x, width_y = checkpoint.shape
    tile_count = snd_column.shape[1]
    capacity = snd_column.shape[2]
    wind_x = padded_2(courant_x, ((("group", "tile"), 1),), 1)
    wind_y = pad_periodic(courant_y, 1, 2)
    tracer = from_behind(checkpoint, "group", 1)
    rimmed = padded_2(tracer, ((("group", "tile"), 1),), 2)
    tracer = vertical_mix(horizontal(rimmed, wind_x, wind_y), mixing)
    states = [tracer]
    moment = 1
    rimmed = padded_2(tracer, ((("group", "tile"), 1),), 2)
    tracer = vertical_mix(horizontal(rimmed, wind_x, wind_y), mixing)
    states.append(tracer)
    position = lax.broadcasted_iota(jnp.int32, snd_column.shape, 2)
    weight = jnp.where(position < snd_count[:, :, None], snd_weight, jnp.zeros_like(snd_weight))
    values, weights, kernels = in_one_piece((snd_value, weight, snd_kernel), "tile", 1, 0, 2)
    columns, step_ids = sent_together((snd_column, snd_step), "tile", 1, 0, 2)
    values = values.reshape(tile_count, capacity)
    weights = weights.reshape(tile_count, capacity)
    kernels = kernels.reshape(tile_count, levels, capacity)
    step_ids = step_ids.reshape(tile_count, capacity)
    cell_index = columns.reshape(-1)
    forcings = []
    for moment in range(STEPS):
        flattened = states[moment].reshape(levels, -1)
        picked = jnp.take(flattened, cell_index, axis=1).reshape(levels, tile_count, capacity)
        observed = jnp.einsum("ltc,tlc->tc", picked, kernels, precision=lax.Precision.HIGHEST)
        misfit = jnp.where(
            step_ids == moment, weights * (observed - values), jnp.zeros_like(observed)
        )
        contribution = jnp.einsum(
            "tlc,tc->ltc", kernels, misfit, precision=lax.Precision.HIGHEST
        ).reshape(levels, -1)
        forcing = (
            jnp.zeros((levels, width_x * width_y), jnp.float32).at[:, cell_index].add(contribution)
        )
        forcings.append(forcing.reshape(levels, width_x, width_y))
    adjoint = adjoint_in
    for moment in reversed(range(STEPS)):
        adjoint = vertical_mix(adjoint + forcings[moment], mixing)
        adjoint = sweep_adjoint(pad_periodic(adjoint, 2, 2), wind_y, 2)
        rimmed = with_halo(adjoint, ((("group", "tile"), 1),), 2)
        adjoint = sweep_adjoint(rimmed, wind_x, 1)
    return adjoint


def solution(mesh):
    return jax.shard_map(
        on_device,
        mesh=mesh,
        in_specs=(
            P(None, ("group", "tile"), None),
            P(None, ("group", "tile"), None),
            P(None, ("group", "tile"), None),
            P(None, ("group", "tile"), None),
            P(None, ("group", "tile"), None),
            P(("group", "tile"), None, None),
            P(("group", "tile"), None),
            P(("group", "tile"), None, None),
            P(("group", "tile"), None, None),
            P(("group", "tile"), None, None),
            P(("group", "tile"), None, None, None),
        ),
        out_specs=P(None, ("group", "tile"), None),
        check_vma=False,
    )
```

profile of v0, /device:TPU:24, one launch (start us, length us, event | category | flops | bytes accessed | tf_op | source)
XLA Modules:
  0.0 234.7 jit_solution(15322854228403738455)
XLA Ops:
  0.0 1.9 fusion.52
  1.9 3.8 %collective-permute-start.1 = (f32[16,1,768]{2,1,0:T(1,128)S(1)}, f32[16,1,768]{2,1,0:T(1,128)S(1)}, u32[]{:S(2)}, u32[]{:S(2)}) collective-permute-start(f32[16,1,768]{2,1,0:T(1,128)S(1)} %get-tuple-element.13), channel_id=1, source_target_pairs={{0,1},{1,2},{2,3},{3,4},{4,5},{5,6},{6,7},{7,8},{8,9},{9,10},{10,1... | collective-permute-start | bytes 147464 | tf_op jit(solution)/shard_map/ppermute | solution.py:17
  5.7 1.9 collective-permute-start
  7.6 0.7 pad_add_fusion
  8.4 0.6 copy.29
  9.0 17.2 %all-to-all-start = ((s32[1,32,256]{2,0,1:T(1,128)}), s32[1,32,256]{2,0,1:T(1,128)S(1)}, u32[]{:S(2)}, u32[]{:S(2)}) async-start(s32[1,32,256]{2,0,1:T(1,128)} %copy.29), calls=%async_computation | async-start | bytes 65536 | tf_op jit(solution)/shard_map/all_to_all | solution.py:53
  26.2 0.8 compare_select_fusion.1
  27.0 1.9 pad_maximum_fusion.20
  29.0 12.8 %all-to-all-done = s32[1,32,256]{2,0,1:T(1,128)S(1)} async-done(((s32[1,32,256]{2,0,1:T(1,128)}), s32[1,32,256]{2,0,1:T(1,128)S(1)}, u32[]{:S(2)}, u32[]{:S(2)}) %all-to-all-start) | async-done | bytes 32800 | tf_op jit(solution)/shard_map/all_to_all | solution.py:53
  41.8 4.6 %all-to-all-start.1 = ((f32[1,32,2304]{2,0,1:T(1,128)}), f32[1,32,2304]{2,0,1:T(1,128)}, u32[]{:S(2)}, u32[]{:S(2)}) async-start(f32[1,32,2304]{2,0,1:T(1,128)} %pad_maximum_fusion.20), calls=%async_computation.1 | async-start | bytes 589824 | tf_op jit(solution)/shard_map/all_to_all | solution.py:39
  47.2 6.7 %collective-permute-start.2 = (f32[16,2,768]{2,1,0:T(2,128)S(1)}, f32[16,2,768]{2,1,0:T(2,128)S(1)}, u32[]{:S(2)}, u32[]{:S(2)}) collective-permute-start(f32[16,2,768]{2,1,0:T(2,128)S(1)} %get-tuple-element.26), channel_id=1, source_target_pairs={{1,0},{2,1},{3,2},{4,3},{5,4},{6,5},{7,6},{8,7},{9,8},{10,9},{11,1... | collective-permute-start | bytes 294920 | tf_op jit(solution)/shard_map/ppermute | solution.py:18
  53.8 1.9 collective-permute-start.3
  55.8 7.0 %collective-permute-done.2 = f32[16,2,768]{2,1,0:T(2,128)S(1)} collective-permute-done((f32[16,2,768]{2,1,0:T(2,128)S(1)}, f32[16,2,768]{2,1,0:T(2,128)S(1)}, u32[]{:S(2)}, u32[]{:S(2)}) %collective-permute-start.2) | collective-permute-done | bytes 98336 | tf_op jit(solution)/shard_map/ppermute | solution.py:18
  62.8 4.2 %collective-permute-done.3 = f32[16,2,768]{2,1,0:T(2,128)S(1)} collective-permute-done((f32[16,2,768]{2,1,0:T(2,128)S(1)}, f32[16,2,768]{2,1,0:T(2,128)S(1)}, u32[]{:S(2)}, u32[]{:S(2)}) %collective-permute-start.3) | collective-permute-done | bytes 98336 | tf_op jit(solution)/shard_map/ppermute | solution.py:17
  67.9 0.8 fusion.29
  69.0 0.8 copy-done.2
  70.0 0.7 fusion.57
  70.7 2.4 %collective-permute-start.4 = (f32[16,2,768]{2,1,0:T(2,128)}, f32[16,2,768]{2,1,0:T(2,128)S(1)}, u32[]{:S(2)}, u32[]{:S(2)}) collective-permute-start(f32[16,2,768]{2,1,0:T(2,128)} %get-tuple-element.22), channel_id=1, source_target_pairs={{1,0},{2,1},{3,2},{4,3},{5,4},{6,5},{7,6},{8,7},{9,8},{10,9},{11,1... | collective-permute-start | bytes 294920 | tf_op jit(solution)/shard_map/ppermute | solution.py:18
  73.1 3.5 %collective-permute-start.5 = (f32[16,2,768]{2,1,0:T(2,128)}, f32[16,2,768]{2,1,0:T(2,128)}, u32[]{:S(2)}, u32[]{:S(2)}) collective-permute-start(f32[16,2,768]{2,1,0:T(2,128)} %get-tuple-element.23), channel_id=1, source_target_pairs={{0,1},{1,2},{2,3},{3,4},{4,5},{5,6},{6,7},{7,8},{8,9},{9,10},{10,1... | collective-permute-start | bytes 294920 | tf_op jit(solution)/shard_map/ppermute | solution.py:17
  77.2 4.0 %copy.36 = f32[16,16,768]{0,2,1:T(8,128)} copy(f32[16,16,768]{2,1,0:T(8,128)S(1)} %pad_subtract_fusion.3) | data formatting | bytes 1572864 | tf_op jit(solution)/shard_map/sub | solution.py:135
  81.2 16.9 %gather_fusion.1 = f32[4096,16]{1,0:T(8,128)} fusion(f32[16,12288]{0,1:T(8,128)} %bitcast.67, s32[4096]{0:T(1024)S(1)} %fusion.49), kind=kCustom, calls=%fused_computation.1.clone | custom fusion | bytes 540672 | tf_op jit(solution)/shard_map/jit(_take)/gather | solution.py:184
  98.0 1.5 fusion.10
  99.9 0.8 fusion.24
  101.3 4.0 %copy.33 = f32[16,16,768]{0,2,1:T(8,128)} copy(f32[16,16,768]{2,1,0:T(8,128)S(1)} %pad_subtract_fusion.2) | data formatting | bytes 1572864 | tf_op jit(solution)/shard_map/sub | solution.py:135
  105.3 16.9 %gather_fusion = f32[4096,16]{1,0:T(8,128)} fusion(f32[16,12288]{0,1:T(8,128)} %bitcast.66, s32[4096]{0:T(1024)S(1)} %fusion.49), kind=kCustom, calls=%fused_computation.clone | custom fusion | bytes 540672 | tf_op jit(solution)/shard_map/jit(_take)/gather | solution.py:184
  122.1 3.9 %broadcast_select_fusion = (f32[4096,16]{1,0:T(8,128)}, f32[4096,16]{1,0:T(8,128)}) fusion(f32[4096,16]{1,0:T(8,128)} %gather_fusion.1, pred[4096]{0:T(1024)(128)(4,1)S(1)} %copy-done.4, f32[4096,16]{1,0:T(8,128)} %gather_fusion), kind=kLoop, calls=%fused_computation.34 | loop fusion | flops 131072 | bytes 1052672 | tf_op jit(solution)/shard_map/jit(_take)/select_n | solution.py:184
  126.0 2.2 copy.44
  128.2 2.2 copy.50
  130.3 1.0 copy.56
  131.6 0.7 bitcast_multiply_fusion.1
  132.3 2.0 copy.34
  134.3 25.7 %scatter_custom_fusion = f32[16,12288]{0,1:T(8,128)} fusion(s32[4096]{0:T(1024)} %bitcast.85, f32[4096,16]{1,0:T(8,128)} %bitcast.71, f32[]{:T(128)} %constant.15.clone.1), kind=kCustom, calls=%fused_computation.6 | custom fusion | flops 65536 | bytes 786944 | tf_op jit(solution)/shard_map/scatter-add | solution.py:193
  160.0 4.5 %copy.35 = f32[16,16,768]{2,1,0:T(8,128)S(1)} copy(f32[16,16,768]{0,2,1:T(8,128)} %bitcast.65) | data formatting | bytes 1572864 | tf_op jit(solution)/shard_map/reshape | solution.py:195
  164.4 1.2 add.114
  166.0 0.6 fusion.21
  167.1 0.7 fusion.53
  167.8 6.3 %collective-permute-start.7 = (f32[16,2,768]{2,1,0:T(2,128)}, f32[16,2,768]{2,1,0:T(2,128)S(1)}, u32[]{:S(2)}, u32[]{:S(2)}) collective-permute-start(f32[16,2,768]{2,1,0:T(2,128)} %get-tuple-element.15), channel_id=1, source_target_pairs={{1,0},{2,1},{3,2},{4,3},{5,4},{6,5},{7,6},{8,7},{9,8},{10,9},{11,1... | collective-permute-start | bytes 294920 | tf_op jit(solution)/shard_map/ppermute | solution.py:72
  174.1 1.9 collective-permute-start.8
  176.1 7.9 %collective-permute-start.6 = (f32[16,1,768]{2,1,0:T(1,128)}, f32[16,1,768]{2,1,0:T(1,128)S(1)}, u32[]{:S(2)}, u32[]{:S(2)}) collective-permute-start(f32[16,1,768]{2,1,0:T(1,128)} %get-tuple-element.12), channel_id=1, source_target_pairs={{1,0},{2,1},{3,2},{4,3},{5,4},{6,5},{7,6},{8,7},{9,8},{10,9},{11,1... | collective-permute-start | bytes 147464 | tf_op jit(solution)/shard_map/ppermute | solution.py:18
  183.9 2.9 %copy.37 = f32[16,32,128]{0,2,1:T(8,128)} copy(f32[16,32,128]{2,0,1:T(8,128)} %bitcast.74) | data formatting | bytes 524288 | tf_op jit(solution)/shard_map/tlc,tc->ltc/transpose | solution.py:189
  186.9 25.7 %scatter_custom_fusion.1 = f32[16,12288]{0,1:T(8,128)} fusion(s32[4096]{0:T(1024)} %bitcast.86, f32[4096,16]{1,0:T(8,128)} %bitcast.70, f32[]{:T(128)} %constant.15.clone.1), kind=kCustom, calls=%fused_computation.4 | custom fusion | flops 65536 | bytes 786944 | tf_op jit(solution)/shard_map/scatter-add | solution.py:193
  212.5 5.3 %copy.38 = f32[16,16,768]{2,1,0:T(8,128)} copy(f32[16,16,768]{0,2,1:T(8,128)} %bitcast.64) | data formatting | bytes 1572864 | tf_op jit(solution)/shard_map/reshape | solution.py:195
  217.9 1.4 fusion.7
  219.9 0.7 fusion.19
  221.1 1.9 collective-permute-start.10
  223.1 7.9 %collective-permute-start.9 = (f32[16,2,768]{2,1,0:T(2,128)S(1)}, f32[16,2,768]{2,1,0:T(2,128)S(1)}, u32[]{:S(2)}, u32[]{:S(2)}) collective-permute-start(f32[16,2,768]{2,1,0:T(2,128)S(1)} %get-tuple-element.9), channel_id=1, source_target_pairs={{1,0},{2,1},{3,2},{4,3},{5,4},{6,5},{7,6},{8,7},{9,8},{10,9},{11,1... | collective-permute-start | bytes 294920 | tf_op jit(solution)/shard_map/ppermute | solution.py:72
  231.5 1.6 collective-permute-done.9
  233.6 1.1 fusion.33
  (51 shorter events, 6.8 us)
Async XLA Ops:
  0.0 28.9 %copy-start = (f32[16,16,768]{2,1,0:T(8,128)S(1)}, f32[16,16,768]{2,1,0:T(8,128)}, u32[]{:S(2)}) copy-start(f32[16,16,768]{2,1,0:T(8,128)} %param.16) | copy-start | bytes 2359300
  1.9 53.9 %collective-permute-start.1 = (f32[16,1,768]{2,1,0:T(1,128)S(1)}, f32[16,1,768]{2,1,0:T(1,128)S(1)}, u32[]{:S(2)}, u32[]{:S(2)}) collective-permute-start(f32[16,1,768]{2,1,0:T(1,128)S(1)} %get-tuple-element.13), channel_id=1, source_target_pairs={{0,1},{1,2},{2,3},{3,4},{4,5},{5,6},{6,7},{7,8},{8,9},{9,10},{10,1... | collective-permute-start | bytes 147464 | tf_op jit(solution)/shard_map/ppermute | solution.py:17
  5.7 41.4 %collective-permute-start = (f32[16,16,768]{2,1,0:T(8,128)}, f32[16,16,768]{2,1,0:T(8,128)S(1)}, u32[]{:S(2)}, u32[]{:S(2)}) collective-permute-start(f32[16,16,768]{2,1,0:T(8,128)} %param.13), channel_id=1, source_target_pairs={{480,0},{0,32},{32,64},{64,96},{96,128},{128,160},{160,192},{192,2... | collective-permute-start | bytes 2359304 | tf_op jit(solution)/shard_map/ppermute | solution.py:32
  9.0 58.0 %copy-start.1 = (f32[16,16,768]{2,1,0:T(8,128)S(1)}, f32[16,16,768]{2,1,0:T(8,128)}, u32[]{:S(2)}) copy-start(f32[16,16,768]{2,1,0:T(8,128)} %param.15) | copy-start | bytes 2359300
  9.0 32.8 %all-to-all-start = ((s32[1,32,256]{2,0,1:T(1,128)}), s32[1,32,256]{2,0,1:T(1,128)S(1)}, u32[]{:S(2)}, u32[]{:S(2)}) async-start(s32[1,32,256]{2,0,1:T(1,128)} %copy.29), calls=%async_computation | async-start | bytes 65536 | tf_op jit(solution)/shard_map/all_to_all | solution.py:53
  41.8 88.5 %all-to-all-start.1 = ((f32[1,32,2304]{2,0,1:T(1,128)}), f32[1,32,2304]{2,0,1:T(1,128)}, u32[]{:S(2)}, u32[]{:S(2)}) async-start(f32[1,32,2304]{2,0,1:T(1,128)} %pad_maximum_fusion.20), calls=%async_computation.1 | async-start | bytes 589824 | tf_op jit(solution)/shard_map/all_to_all | solution.py:39
  47.2 15.7 %collective-permute-start.2 = (f32[16,2,768]{2,1,0:T(2,128)S(1)}, f32[16,2,768]{2,1,0:T(2,128)S(1)}, u32[]{:S(2)}, u32[]{:S(2)}) collective-permute-start(f32[16,2,768]{2,1,0:T(2,128)S(1)} %get-tuple-element.26), channel_id=1, source_target_pairs={{1,0},{2,1},{3,2},{4,3},{5,4},{6,5},{7,6},{8,7},{9,8},{10,9},{11,1... | collective-permute-start | bytes 294920 | tf_op jit(solution)/shard_map/ppermute | solution.py:18
  53.8 13.2 %collective-permute-start.3 = (f32[16,2,768]{2,1,0:T(2,128)S(1)}, f32[16,2,768]{2,1,0:T(2,128)S(1)}, u32[]{:S(2)}, u32[]{:S(2)}) collective-permute-start(f32[16,2,768]{2,1,0:T(2,128)S(1)} %get-tuple-element.27), channel_id=1, source_target_pairs={{0,1},{1,2},{2,3},{3,4},{4,5},{5,6},{6,7},{7,8},{8,9},{9,10},{10,1... | collective-permute-start | bytes 294920 | tf_op jit(solution)/shard_map/ppermute | solution.py:17
  68.7 1.1 copy-start.2
  70.7 27.3 %collective-permute-start.4 = (f32[16,2,768]{2,1,0:T(2,128)}, f32[16,2,768]{2,1,0:T(2,128)S(1)}, u32[]{:S(2)}, u32[]{:S(2)}) collective-permute-start(f32[16,2,768]{2,1,0:T(2,128)} %get-tuple-element.22), channel_id=1, source_target_pairs={{1,0},{2,1},{3,2},{4,3},{5,4},{6,5},{7,6},{8,7},{9,8},{10,9},{11,1... | collective-permute-start | bytes 294920 | tf_op jit(solution)/shard_map/ppermute | solution.py:18
  73.1 24.9 %collective-permute-start.5 = (f32[16,2,768]{2,1,0:T(2,128)}, f32[16,2,768]{2,1,0:T(2,128)}, u32[]{:S(2)}, u32[]{:S(2)}) collective-permute-start(f32[16,2,768]{2,1,0:T(2,128)} %get-tuple-element.23), channel_id=1, source_target_pairs={{0,1},{1,2},{2,3},{3,4},{4,5},{5,6},{6,7},{7,8},{8,9},{9,10},{10,1... | collective-permute-start | bytes 294920 | tf_op jit(solution)/shard_map/ppermute | solution.py:17
  105.3 16.9 %copy-start.4 = (pred[4096]{0:T(1024)(128)(4,1)S(1)}, pred[4096]{0:T(1024)(128)(4,1)}, u32[]{:S(2)}) copy-start(pred[4096]{0:T(1024)(128)(4,1)} %compare_and_fusion) | copy-start | bytes 12292
  167.8 50.0 %collective-permute-start.7 = (f32[16,2,768]{2,1,0:T(2,128)}, f32[16,2,768]{2,1,0:T(2,128)S(1)}, u32[]{:S(2)}, u32[]{:S(2)}) collective-permute-start(f32[16,2,768]{2,1,0:T(2,128)} %get-tuple-element.15), channel_id=1, source_target_pairs={{1,0},{2,1},{3,2},{4,3},{5,4},{6,5},{7,6},{8,7},{9,8},{10,9},{11,1... | collective-permute-start | bytes 294920 | tf_op jit(solution)/shard_map/ppermute | solution.py:72
  174.1 43.7 %collective-permute-start.8 = (f32[16,2,768]{2,1,0:T(2,128)}, f32[16,2,768]{2,1,0:T(2,128)}, u32[]{:S(2)}, u32[]{:S(2)}) collective-permute-start(f32[16,2,768]{2,1,0:T(2,128)} %get-tuple-element.14), channel_id=1, source_target_pairs={{0,1},{1,2},{2,3},{3,4},{4,5},{5,6},{6,7},{7,8},{8,9},{9,10},{10,1... | collective-permute-start | bytes 294920 | tf_op jit(solution)/shard_map/ppermute | solution.py:69
  176.1 41.8 %collective-permute-start.6 = (f32[16,1,768]{2,1,0:T(1,128)}, f32[16,1,768]{2,1,0:T(1,128)S(1)}, u32[]{:S(2)}, u32[]{:S(2)}) collective-permute-start(f32[16,1,768]{2,1,0:T(1,128)} %get-tuple-element.12), channel_id=1, source_target_pairs={{1,0},{2,1},{3,2},{4,3},{5,4},{6,5},{7,6},{8,7},{9,8},{10,9},{11,1... | collective-permute-start | bytes 147464 | tf_op jit(solution)/shard_map/ppermute | solution.py:18
  217.8 1.4 copy-start.3
  221.1 10.4 %collective-permute-start.10 = (f32[16,2,768]{2,1,0:T(2,128)S(1)}, f32[16,2,768]{2,1,0:T(2,128)S(1)}, u32[]{:S(2)}, u32[]{:S(2)}) collective-permute-start(f32[16,2,768]{2,1,0:T(2,128)S(1)} %get-tuple-element.8), channel_id=1, source_target_pairs={{0,1},{1,2},{2,3},{3,4},{4,5},{5,6},{6,7},{7,8},{8,9},{9,10},{10,1... | collective-permute-start | bytes 294920 | tf_op jit(solution)/shard_map/ppermute | solution.py:69
  223.1 10.1 %collective-permute-start.9 = (f32[16,2,768]{2,1,0:T(2,128)S(1)}, f32[16,2,768]{2,1,0:T(2,128)S(1)}, u32[]{:S(2)}, u32[]{:S(2)}) collective-permute-start(f32[16,2,768]{2,1,0:T(2,128)S(1)} %get-tuple-element.9), channel_id=1, source_target_pairs={{1,0},{2,1},{3,2},{4,3},{5,4},{6,5},{7,6},{8,7},{9,8},{10,9},{11,1... | collective-permute-start | bytes 294920 | tf_op jit(solution)/shard_map/ppermute | solution.py:72
where the time goes:
time: 236 us; the launch traced here: 235 us
  other arithmetic  73.2 us (31%)
  starting transfers between devices  67.8 us (29%)
  local copies, waits for them, and re-layouts  67.2 us (28%)
  waiting for transfers between devices  26.2 us (11%)
    scatter-add x2, other arithmetic, on_device(): jnp.zeros((levels, width_x * width_y), jnp.float32).at[:, cell_index]  51.3 us
    gather x2, local copies, waits for them, and re-layouts, on_device(): jnp.take(flattened, cell_index, axis=1)  33.7 us
    all_to_all x1, starting transfers between devices, sent_together(): lax.all_to_all(both, axis, split_axis=split_dim, concat_axis=concat_dim,...  17.2 us
    ppermute x3, starting transfers between devices, padded_2(): lax.ppermute(initial, axis, [(b, a) for a, b in up])  16.9 us
    ppermute x2, starting transfers between devices, with_halo(): lax.ppermute(lax.slice_in_dim(block, 0, width, axis=dim), axis, backward)  14.2 us
    all_to_all x1, waiting for transfers between devices, sent_together(): lax.all_to_all(both, axis, split_axis=split_dim, concat_axis=concat_dim,...  12.8 us
    reshape x2, local copies, waits for them, and re-layouts, on_device(): forcings.append(forcing.reshape(levels, width_x, width_y))  9.79 us
    ppermute x3, starting transfers between devices, padded_2(): lax.ppermute(last, axis, up)  9.21 us
  transfers between devices with their start and end apart: 13, of which 5 were waited for; matrix products, arithmetic and copies ran while one was open for 41% of the time, Pallas kernels for 0%

commit v1 on v0

--- a/solution.py
+++ b/solution.py
@@ -1,6 +1,8 @@
 import jax
 import jax.numpy as jnp
 from jax import lax
+from jax.experimental import pallas as pl
+from jax.experimental.pallas import tpu as pltpu
 from jax.sharding import PartitionSpec as P
 
 STEPS = 2
@@ -32,34 +34,6 @@
     return lax.ppermute(block, axis, route)
 
 
-def in_one_piece(arrays, axis, split_dim, concat_dim, along):
-    columns = [a.reshape(*a.shape[:along], -1) for a in arrays]
-    both = jnp.concatenate(columns, axis=along)
-    whole, at, gathered = (
-        lax.all_to_all(both, axis, split_axis=split_dim, concat_axis=concat_dim, tiled=True),
-        0,
-        [],
-    )
-    for a, column in zip(arrays, columns):
-        piece = whole[..., at : at + column.shape[along]]
-        gathered.append(piece.reshape(*piece.shape[:along], *a.shape[along:]))
-        at += column.shape[along]
-    return tuple(gathered)
-
-
-def sent_together(arrays, axis, split_dim, concat_dim, along):
-    both = jnp.concatenate(arrays, axis=along)
-    whole, at, gathered = (
-        lax.all_to_all(both, axis, split_axis=split_dim, concat_axis=concat_dim, tiled=True),
-        0,
-        [],
-    )
-    for a in arrays:
-        gathered.append(lax.slice_in_dim(whole, at, at + a.shape[along], axis=along))
-        at += a.shape[along]
-    return tuple(gathered)
-
-
 def with_halo(block, sides, width):
     for axis, dim in sides:
         count = lax.axis_size(axis)
@@ -141,6 +115,95 @@
 def horizontal(rimmed, wind_x, wind_y):
     swept = sweep_forward(rimmed, wind_x, 1)
     return sweep_forward(pad_periodic(swept, 2, 2), wind_y, 2)
+
+
+SLOT_ROWS = 1536
+
+
+def sounding_kernel(row_ref, state_0, state_1, box, forcing_0, forcing_1, table, taken, spread, *sums):
+    tiles = box.shape[0]
+
+    def to_rows(i, carry):
+        off = pl.multiple_of(i * 128, 128)
+        for s, ref in enumerate((state_0, state_1)):
+            for h in range(2):
+                block = ref[:, h * 8 : h * 8 + 8, pl.ds(off, 128)].reshape(128, 128)
+                at = pl.multiple_of(s * SLOT_ROWS + h * 768 + off, 128)
+                table[pl.ds(at, 128), :] = block.T
+        return carry
+
+    lax.fori_loop(0, 6, to_rows, 0)
+
+    def clear(i, carry):
+        for acc in sums:
+            acc[pl.ds(pl.multiple_of(i * 128, 128), 128), :] = jnp.zeros((128, 128), jnp.float32)
+        return carry
+
+    lax.fori_loop(0, 24, clear, 0)
+
+    def gather(t, carry):
+        base = pl.multiple_of(t * 128, 128)
+        for k in range(128):
+            taken[pl.ds(base + k, 1), :] = table[pl.ds(row_ref[base + k], 1), :]
+        return carry
+
+    lax.fori_loop(0, tiles, gather, 0)
+    sub = lax.broadcasted_iota(jnp.int32, (8, 128), 0)
+
+    def observe(t, carry):
+        at = pl.ds(pl.multiple_of(t * 128, 128), 128)
+        cells = taken[at, :].T
+        rows = [box[t, :, f * 128 : f * 128 + 128] for f in range(18)]
+        total = cells[0:8, :] * rows[0]
+        for level in range(1, 16):
+            total = total + cells[level * 8 : level * 8 + 8, :] * rows[level]
+        lane = rows[17].astype(jnp.int32)
+        own = sub == (lane // 768) % 8
+        observed = jnp.sum(jnp.where(own, total, 0.0), axis=0, keepdims=True)
+        misfit = jnp.where(own, jnp.broadcast_to(observed - rows[16], (8, 128)), 0.0)
+        out = jnp.concatenate([misfit * rows[level] for level in range(16)], axis=0)
+        spread[at, :] = out.T
+        return carry
+
+    lax.fori_loop(0, tiles, observe, 0)
+
+    def scatter(t, carry):
+        base = pl.multiple_of(t * 128, 128)
+        for k in range(128):
+            acc = sums[k % len(sums)]
+            at = pl.ds(row_ref[base + k], 1)
+            acc[at, :] = acc[at, :] + spread[pl.ds(base + k, 1), :]
+        return carry
+
+    lax.fori_loop(0, tiles, scatter, 0)
+
+    def back(i, carry):
+        off = pl.multiple_of(i * 128, 128)
+        for s, ref in enumerate((forcing_0, forcing_1)):
+            for h in range(2):
+                at = pl.ds(pl.multiple_of(s * SLOT_ROWS + h * 768 + off, 128), 128)
+                block = sums[0][at, :]
+                for acc in sums[1:]:
+                    block = block + acc[at, :]
+                ref[:, h * 8 : h * 8 + 8, pl.ds(off, 128)] = block.T.reshape(16, 8, 128)
+        return carry
+
+    lax.fori_loop(0, 6, back, 0)
+
+
+def forcings_of(row, state_0, state_1, box):
+    vmem = pl.BlockSpec(memory_space=pltpu.VMEM)
+    slots = box.shape[0] * 128
+    return pl.pallas_call(
+        sounding_kernel,
+        out_shape=(jax.ShapeDtypeStruct(state_0.shape, jnp.float32),) * 2,
+        in_specs=[pl.BlockSpec(memory_space=pltpu.SMEM), vmem, vmem, vmem],
+        out_specs=(vmem, vmem),
+        scratch_shapes=[pltpu.VMEM((2 * SLOT_ROWS, 128), jnp.float32)]
+        + [pltpu.VMEM((slots, 128), jnp.float32)] * 2
+        + [pltpu.VMEM((2 * SLOT_ROWS, 128), jnp.float32)] * 8,
+        compiler_params=pltpu.CompilerParams(vmem_limit_bytes=48 * 2**20),
+    )(row, state_0, state_1, box)
 
 
 def on_device(
@@ -171,28 +234,22 @@
     states.append(tracer)
     position = lax.broadcasted_iota(jnp.int32, snd_column.shape, 2)
     weight = jnp.where(position < snd_count[:, :, None], snd_weight, jnp.zeros_like(snd_weight))
-    values, weights, kernels = in_one_piece((snd_value, weight, snd_kernel), "tile", 1, 0, 2)
-    columns, step_ids = sent_together((snd_column, snd_step), "tile", 1, 0, 2)
-    values = values.reshape(tile_count, capacity)
-    weights = weights.reshape(tile_count, capacity)
-    kernels = kernels.reshape(tile_count, levels, capacity)
-    step_ids = step_ids.reshape(tile_count, capacity)
-    cell_index = columns.reshape(-1)
-    forcings = []
-    for moment in range(STEPS):
-        flattened = states[moment].reshape(levels, -1)
-        picked = jnp.take(flattened, cell_index, axis=1).reshape(levels, tile_count, capacity)
-        observed = jnp.einsum("ltc,tlc->tc", picked, kernels, precision=lax.Precision.HIGHEST)
-        misfit = jnp.where(
-            step_ids == moment, weights * (observed - values), jnp.zeros_like(observed)
-        )
-        contribution = jnp.einsum(
-            "tlc,tc->ltc", kernels, misfit, precision=lax.Precision.HIGHEST
-        ).reshape(levels, -1)
-        forcing = (
-            jnp.zeros((levels, width_x * width_y), jnp.float32).at[:, cell_index].add(contribution)
-        )
-        forcings.append(forcing.reshape(levels, width_x, width_y))
+    root = jnp.sqrt(weight)
+    packed = jnp.concatenate(
+        [
+            (snd_kernel * root[:, :, None, :]).reshape(tile_count, 1, levels * capacity),
+            (snd_value * root).reshape(tile_count, 1, capacity),
+            snd_column.astype(jnp.float32).reshape(tile_count, 1, capacity),
+            snd_step.astype(jnp.float32).reshape(tile_count, 1, capacity),
+        ],
+        axis=2,
+    )
+    box = lax.all_to_all(packed, "tile", split_axis=0, concat_axis=0, tiled=True)
+    fields = box.reshape(tile_count, -1)
+    column = fields[:, 17 * capacity : 18 * capacity].astype(jnp.int32)
+    step = fields[:, 18 * capacity :].astype(jnp.int32)
+    row = step * SLOT_ROWS + column // (8 * width_y) * width_y + column % width_y
+    forcings = forcings_of(row.reshape(-1), states[0], states[1], box)
     adjoint = adjoint_in
     for moment in reversed(range(STEPS)):
         adjoint = vertical_mix(adjoint + forcings[moment], mixing)

time: 236 us -> 130 us (0.55)
  other arithmetic: 73.2 us -> 11.9 us
  local copies, waits for them, and re-layouts: 67.2 us -> 6.49 us
  Pallas kernels: 0 us -> 17 us
  starting transfers between devices: 67.8 us -> 53.1 us
  waiting for transfers between devices: 26.2 us -> 40.8 us
    scatter-add x2 -> x0, other arithmetic: 51.3 us -> none  [on_device(): jnp.zeros((levels, width_x * width_y), jnp.float32).at[:, cell_index]]
    gather x2 -> x0, local copies, waits for them, and re-layouts: 33.7 us -> none  [on_device(): jnp.take(flattened, cell_index, axis=1)]
    pallas_call x0 -> x1, Pallas kernels: none -> 17 us  [forcings_of(): pl.pallas_call(sounding_kernel, out_shape=(jax.ShapeDtypeStruct(state_0.s...]
    all_to_all x2 -> x1, starting transfers between devices: 21.8 us -> 6.24 us  [on_device(): lax.all_to_all(packed, 'tile', split_axis=0, concat_axis=0, tiled=True)]
    reshape x2 -> x0, local copies, waits for them, and re-layouts: 9.79 us -> none  [on_device(): forcings.append(forcing.reshape(levels, width_x, width_y))]
    all_to_all x2 -> x1, waiting for transfers between devices: 12.8 us -> 20.9 us  [on_device(): lax.all_to_all(packed, 'tile', split_axis=0, concat_axis=0, tiled=True)]
    sub x2 -> x0, local copies, waits for them, and re-layouts: 7.99 us -> none  [vertical_mix(): field + jnp.concatenate([fluxes, zero_row], axis=0)]
    ppermute x1, waiting for transfers between devices: 0.01 us -> 5.65 us  [from_behind(): return lax.ppermute(block, axis, route)]
  transfers between devices with their start and end apart: 13 -> 12, of which waited for: 5 -> 7; matrix products, arithmetic and copies ran while one was open for 41% -> 5% of each run, Pallas kernels for 0% -> 0%
where the time goes in v1:
time: 130 us
  starting transfers between devices  53.1 us (41%)
  waiting for transfers between devices  40.8 us (31%)
  Pallas kernels  17 us (13%)
  other arithmetic  11.9 us (9%)
  local copies, waits for them, and re-layouts  6.49 us (5%)
    all_to_all x1, waiting for transfers between devices, on_device(): lax.all_to_all(packed, 'tile', split_axis=0, concat_axis=0, tiled=True)  20.9 us
    pallas_call x1, Pallas kernels, forcings_of(): pl.pallas_call(sounding_kernel, out_shape=(jax.ShapeDtypeStruct(state_0.s...  17 us
    ppermute x3, starting transfers between devices, padded_2(): lax.ppermute(initial, axis, [(b, a) for a, b in up])  15.6 us
    ppermute x2, starting transfers between devices, with_halo(): lax.ppermute(lax.slice_in_dim(block, 0, width, axis=dim), axis, backward)  15.6 us
    ppermute x3, starting transfers between devices, padded_2(): lax.ppermute(last, axis, up)  9.67 us
    ppermute x3, waiting for transfers between devices, padded_2(): lax.ppermute(last, axis, up)  7.97 us
    all_to_all x1, starting transfers between devices, on_device(): lax.all_to_all(packed, 'tile', split_axis=0, concat_axis=0, tiled=True)  6.24 us
    ppermute x1, waiting for transfers between devices, from_behind(): return lax.ppermute(block, axis, route)  5.65 us
  transfers between devices with their start and end apart: 12, of which 7 were waited for; matrix products, arithmetic and copies ran while one was open for 5% of the time, Pallas kernels for 0%

profile of v1, /device:TPU:24, one launch (start us, length us, event | category | flops | bytes accessed | tf_op | source)
XLA Modules:
  0.0 129.7 jit_solution(12233797365087827700)
XLA Ops:
  0.0 2.1 %collective-permute-start = (f32[16,16,768]{2,1,0:T(8,128)}, f32[16,16,768]{2,1,0:T(8,128)S(1)}, u32[]{:S(2)}, u32[]{:S(2)}) collective-permute-start(f32[16,16,768]{2,1,0:T(8,128)} %param.11), channel_id=1, source_target_pairs={{480,0},{0,32},{32,64},{64,96},{96,128},{128,160},{160,192},{192,2... | collective-permute-start | bytes 2359304 | tf_op jit(solution)/shard_map/ppermute | solution.py:34
  2.1 1.2 fusion.55
  3.3 3.8 %collective-permute-start.1 = (f32[16,1,768]{2,1,0:T(1,128)S(1)}, f32[16,1,768]{2,1,0:T(1,128)S(1)}, u32[]{:S(2)}, u32[]{:S(2)}) collective-permute-start(f32[16,1,768]{2,1,0:T(1,128)S(1)} %get-tuple-element.14), channel_id=1, source_target_pairs={{0,1},{1,2},{2,3},{3,4},{4,5},{5,6},{6,7},{7,8},{8,9},{9,10},{10,1... | collective-permute-start | bytes 147464 | tf_op jit(solution)/shard_map/ppermute | solution.py:19
  7.1 0.8 fusion.52
  7.9 1.0 broadcast_multiply_fusion
  8.9 5.7 %collective-permute-done = f32[16,16,768]{2,1,0:T(8,128)S(1)} collective-permute-done((f32[16,16,768]{2,1,0:T(8,128)}, f32[16,16,768]{2,1,0:T(8,128)S(1)}, u32[]{:S(2)}, u32[]{:S(2)}) %collective-permute-start) | collective-permute-done | bytes 786464 | tf_op jit(solution)/shard_map/ppermute | solution.py:34
  14.6 11.8 %collective-permute-start.2 = (f32[16,2,768]{2,1,0:T(2,128)S(1)}, f32[16,2,768]{2,1,0:T(2,128)S(1)}, u32[]{:S(2)}, u32[]{:S(2)}) collective-permute-start(f32[16,2,768]{2,1,0:T(2,128)S(1)} %get-tuple-element.27), channel_id=1, source_target_pairs={{1,0},{2,1},{3,2},{4,3},{5,4},{6,5},{7,6},{8,7},{9,8},{10,9},{11,1... | collective-permute-start | bytes 294920 | tf_op jit(solution)/shard_map/ppermute | solution.py:20
  26.4 1.9 %collective-permute-start.3 = (f32[16,2,768]{2,1,0:T(2,128)S(1)}, f32[16,2,768]{2,1,0:T(2,128)S(1)}, u32[]{:S(2)}, u32[]{:S(2)}) collective-permute-start(f32[16,2,768]{2,1,0:T(2,128)S(1)} %get-tuple-element.28), channel_id=1, source_target_pairs={{0,1},{1,2},{2,3},{3,4},{4,5},{5,6},{6,7},{7,8},{8,9},{9,10},{10,1... | collective-permute-start | bytes 294920 | tf_op jit(solution)/shard_map/ppermute | solution.py:19
  28.4 0.7 fusion.57
  29.1 7.7 %collective-permute-done.3 = f32[16,2,768]{2,1,0:T(2,128)S(1)} collective-permute-done((f32[16,2,768]{2,1,0:T(2,128)S(1)}, f32[16,2,768]{2,1,0:T(2,128)S(1)}, u32[]{:S(2)}, u32[]{:S(2)}) %collective-permute-start.3) | collective-permute-done | bytes 98336 | tf_op jit(solution)/shard_map/ppermute | solution.py:19
  36.8 0.6 fusion.11
  37.4 0.1 slice_subtract_fusion.7
  37.6 0.8 fusion.25
  38.5 0.3 slice_subtract_fusion.6
  38.8 0.8 copy-done.2
  39.6 0.1 fusion.44
  39.8 1.9 %collective-permute-start.4 = (f32[16,2,768]{2,1,0:T(2,128)S(1)}, f32[16,2,768]{2,1,0:T(2,128)S(1)}, u32[]{:S(2)}, u32[]{:S(2)}) collective-permute-start(f32[16,2,768]{2,1,0:T(2,128)S(1)} %get-tuple-element.23), channel_id=1, source_target_pairs={{1,0},{2,1},{3,2},{4,3},{5,4},{6,5},{7,6},{8,7},{9,8},{10,9},{11,1... | collective-permute-start | bytes 294920 | tf_op jit(solution)/shard_map/ppermute | solution.py:20
  41.8 3.9 %collective-permute-start.5 = (f32[16,2,768]{2,1,0:T(2,128)S(1)}, f32[16,2,768]{2,1,0:T(2,128)S(1)}, u32[]{:S(2)}, u32[]{:S(2)}) collective-permute-start(f32[16,2,768]{2,1,0:T(2,128)S(1)} %get-tuple-element.24), channel_id=1, source_target_pairs={{0,1},{1,2},{2,3},{3,4},{4,5},{5,6},{6,7},{7,8},{8,9},{9,10},{10,1... | collective-permute-start | bytes 294920 | tf_op jit(solution)/shard_map/ppermute | solution.py:19
  45.7 1.0 pad_maximum_fusion.20
  46.7 6.2 %all-to-all-start = ((f32[32,1,2432]{2,1,0:T(1,128)}), f32[32,1,2432]{2,1,0:T(1,128)S(1)}, u32[]{:S(2)}, u32[]{:S(2)}) async-start(f32[32,1,2432]{2,1,0:T(1,128)} %pad_maximum_fusion.20), calls=%async_computation | async-start | bytes 622592 | tf_op jit(solution)/shard_map/all_to_all | solution.py:247
  53.0 0.2 collective-permute-done.5
  53.2 0.6 fusion.6
  53.8 0.2 slice_subtract_fusion.5
  54.0 0.6 copy-done.6
  54.7 0.8 fusion.20
  55.5 0.3 slice_subtract_fusion.4
  55.8 0.8 copy-done.3
  56.6 0.1 fusion.43
  56.8 20.9 %all-to-all-done.box = f32[32,1,2432]{2,1,0:T(1,128)S(1)} async-done(((f32[32,1,2432]{2,1,0:T(1,128)}), f32[32,1,2432]{2,1,0:T(1,128)S(1)}, u32[]{:S(2)}, u32[]{:S(2)}) %all-to-all-start) | async-done | bytes 311328 | tf_op jit(solution)/shard_map/all_to_all | solution.py:247
  77.8 17.0 %shard_map.112 = (f32[16,16,768]{2,1,0:T(8,128)S(1)}, f32[16,16,768]{2,1,0:T(8,128)S(1)}) custom-call(s32[4096]{0:T(1024)S(1)} %fusion.48.row_ref, f32[16,16,768]{2,1,0:T(8,128)S(1)} %pad_subtract_fusion.3.state_0, f32[16,16,768]{2,1,0:T(8,128)S(1)} %pad_subtract_fusion.2.state_1, f32[32,1,2432]{2,1,0:T(1,128)S(1)} %all-to-all-done.box), custom_call_target="tpu_custom_call" | custom-call | tf_op jit(solution)/shard_map/pallas_call | solution.py:197
  94.9 1.0 copy-done.4
  96.2 0.7 copy-done.7
  97.0 0.6 fusion.17
  97.6 0.5 fusion.39
  98.2 2.1 %collective-permute-start.8 = (f32[16,2,768]{2,1,0:T(2,128)S(1)}, f32[16,2,768]{2,1,0:T(2,128)S(1)}, u32[]{:S(2)}, u32[]{:S(2)}) collective-permute-start(f32[16,2,768]{2,1,0:T(2,128)S(1)} %get-tuple-element.15), channel_id=1, source_target_pairs={{0,1},{1,2},{2,3},{3,4},{4,5},{5,6},{6,7},{7,8},{8,9},{9,10},{10,1... | collective-permute-start | bytes 294920 | tf_op jit(solution)/shard_map/ppermute | solution.py:43
  100.2 7.7 %collective-permute-start.7 = (f32[16,2,768]{2,1,0:T(2,128)S(1)}, f32[16,2,768]{2,1,0:T(2,128)S(1)}, u32[]{:S(2)}, u32[]{:S(2)}) collective-permute-start(f32[16,2,768]{2,1,0:T(2,128)S(1)} %get-tuple-element.16), channel_id=1, source_target_pairs={{1,0},{2,1},{3,2},{4,3},{5,4},{6,5},{7,6},{8,7},{9,8},{10,9},{11,1... | collective-permute-start | bytes 294920 | tf_op jit(solution)/shard_map/ppermute | solution.py:46
  108.0 1.9 %collective-permute-start.6 = (f32[16,1,768]{2,1,0:T(1,128)S(1)}, f32[16,1,768]{2,1,0:T(1,128)S(1)}, u32[]{:S(2)}, u32[]{:S(2)}) collective-permute-start(f32[16,1,768]{2,1,0:T(1,128)S(1)} %get-tuple-element.13), channel_id=1, source_target_pairs={{1,0},{2,1},{3,2},{4,3},{5,4},{6,5},{7,6},{8,7},{9,8},{10,9},{11,1... | collective-permute-start | bytes 147464 | tf_op jit(solution)/shard_map/ppermute | solution.py:20
  109.9 4.1 %collective-permute-done.6 = f32[16,1,768]{2,1,0:T(1,128)S(1)} collective-permute-done((f32[16,1,768]{2,1,0:T(1,128)S(1)}, f32[16,1,768]{2,1,0:T(1,128)S(1)}, u32[]{:S(2)}, u32[]{:S(2)}) %collective-permute-start.6) | collective-permute-done | bytes 49184 | tf_op jit(solution)/shard_map/ppermute | solution.py:20
  114.0 0.4 fusion.3
  114.4 0.3 fusion.36
  115.0 0.6 fusion.15
  115.6 0.5 fusion.32
  116.2 1.9 %collective-permute-start.10 = (f32[16,2,768]{2,1,0:T(2,128)S(1)}, f32[16,2,768]{2,1,0:T(2,128)S(1)}, u32[]{:S(2)}, u32[]{:S(2)}) collective-permute-start(f32[16,2,768]{2,1,0:T(2,128)S(1)} %get-tuple-element.9), channel_id=1, source_target_pairs={{0,1},{1,2},{2,3},{3,4},{4,5},{5,6},{6,7},{7,8},{8,9},{9,10},{10,1... | collective-permute-start | bytes 294920 | tf_op jit(solution)/shard_map/ppermute | solution.py:43
  118.1 7.9 %collective-permute-start.9 = (f32[16,2,768]{2,1,0:T(2,128)S(1)}, f32[16,2,768]{2,1,0:T(2,128)S(1)}, u32[]{:S(2)}, u32[]{:S(2)}) collective-permute-start(f32[16,2,768]{2,1,0:T(2,128)S(1)} %get-tuple-element.10), channel_id=1, source_target_pairs={{1,0},{2,1},{3,2},{4,3},{5,4},{6,5},{7,6},{8,7},{9,8},{10,9},{11,1... | collective-permute-start | bytes 294920 | tf_op jit(solution)/shard_map/ppermute | solution.py:46
  126.0 0.4 collective-permute-done.10
  126.3 1.8 %collective-permute-done.9 = f32[16,2,768]{2,1,0:T(2,128)S(1)} collective-permute-done((f32[16,2,768]{2,1,0:T(2,128)S(1)}, f32[16,2,768]{2,1,0:T(2,128)S(1)}, u32[]{:S(2)}, u32[]{:S(2)}) %collective-permute-start.9) | collective-permute-done | bytes 98336 | tf_op jit(solution)/shard_map/ppermute | solution.py:46
  128.2 0.4 fusion.1
  128.6 1.1 fusion.29
  (43 shorter events, 1.4 us)
Async XLA Ops:
  0.0 28.4 %copy-start = (f32[16,16,768]{2,1,0:T(8,128)S(1)}, f32[16,16,768]{2,1,0:T(8,128)}, u32[]{:S(2)}) copy-start(f32[16,16,768]{2,1,0:T(8,128)} %param.14) | copy-start | bytes 2359300
  0.0 36.8 %copy-start.1 = (f32[16,16,768]{2,1,0:T(8,128)S(1)}, f32[16,16,768]{2,1,0:T(8,128)}, u32[]{:S(2)}) copy-start(f32[16,16,768]{2,1,0:T(8,128)} %param.13) | copy-start | bytes 2359300
  0.0 29.0 %copy-start.10 = (s32[1,32,128]{2,1,0:T(8,128)S(1)}, s32[1,32,128]{2,1,0:T(8,128)}, u32[]{:S(2)}) copy-start(s32[1,32,128]{2,1,0:T(8,128)} %param.16) | copy-start | bytes 49156
  0.0 29.0 %copy-start.11 = (s32[1,32,128]{2,1,0:T(8,128)S(1)}, s32[1,32,128]{2,1,0:T(8,128)}, u32[]{:S(2)}) copy-start(s32[1,32,128]{2,1,0:T(8,128)} %param.18) | copy-start | bytes 49156
  0.0 14.5 %collective-permute-start = (f32[16,16,768]{2,1,0:T(8,128)}, f32[16,16,768]{2,1,0:T(8,128)S(1)}, u32[]{:S(2)}, u32[]{:S(2)}) collective-permute-start(f32[16,16,768]{2,1,0:T(8,128)} %param.11), channel_id=1, source_target_pairs={{480,0},{0,32},{32,64},{64,96},{96,128},{128,160},{160,192},{192,2... | collective-permute-start | bytes 2359304 | tf_op jit(solution)/shard_map/ppermute | solution.py:34
  3.3 25.8 %collective-permute-start.1 = (f32[16,1,768]{2,1,0:T(1,128)S(1)}, f32[16,1,768]{2,1,0:T(1,128)S(1)}, u32[]{:S(2)}, u32[]{:S(2)}) collective-permute-start(f32[16,1,768]{2,1,0:T(1,128)S(1)} %get-tuple-element.14), channel_id=1, source_target_pairs={{0,1},{1,2},{2,3},{3,4},{4,5},{5,6},{6,7},{7,8},{8,9},{9,10},{10,1... | collective-permute-start | bytes 147464 | tf_op jit(solution)/shard_map/ppermute | solution.py:19
  14.6 14.4 %collective-permute-start.2 = (f32[16,2,768]{2,1,0:T(2,128)S(1)}, f32[16,2,768]{2,1,0:T(2,128)S(1)}, u32[]{:S(2)}, u32[]{:S(2)}) collective-permute-start(f32[16,2,768]{2,1,0:T(2,128)S(1)} %get-tuple-element.27), channel_id=1, source_target_pairs={{1,0},{2,1},{3,2},{4,3},{5,4},{6,5},{7,6},{8,7},{9,8},{10,9},{11,1... | collective-permute-start | bytes 294920 | tf_op jit(solution)/shard_map/ppermute | solution.py:20
  26.4 10.4 %collective-permute-start.3 = (f32[16,2,768]{2,1,0:T(2,128)S(1)}, f32[16,2,768]{2,1,0:T(2,128)S(1)}, u32[]{:S(2)}, u32[]{:S(2)}) collective-permute-start(f32[16,2,768]{2,1,0:T(2,128)S(1)} %get-tuple-element.28), channel_id=1, source_target_pairs={{0,1},{1,2},{2,3},{3,4},{4,5},{5,6},{6,7},{7,8},{8,9},{9,10},{10,1... | collective-permute-start | bytes 294920 | tf_op jit(solution)/shard_map/ppermute | solution.py:19
  29.0 8.6 %copy-start.5 = (f32[16,16,1]{2,1,0:T(8,128)}, f32[16,16,1]{2,1,0:T(8,128)S(1)}, u32[]{:S(2)}) copy-start(f32[16,16,1]{2,1,0:T(8,128)S(1)} %get-tuple-element.18) | copy-start | bytes 3076
  38.5 1.1 copy-start.2
  39.8 13.1 %collective-permute-start.4 = (f32[16,2,768]{2,1,0:T(2,128)S(1)}, f32[16,2,768]{2,1,0:T(2,128)S(1)}, u32[]{:S(2)}, u32[]{:S(2)}) collective-permute-start(f32[16,2,768]{2,1,0:T(2,128)S(1)} %get-tuple-element.23), channel_id=1, source_target_pairs={{1,0},{2,1},{3,2},{4,3},{5,4},{6,5},{7,6},{8,7},{9,8},{10,9},{11,1... | collective-permute-start | bytes 294920 | tf_op jit(solution)/shard_map/ppermute | solution.py:20
  41.8 11.4 %collective-permute-start.5 = (f32[16,2,768]{2,1,0:T(2,128)S(1)}, f32[16,2,768]{2,1,0:T(2,128)S(1)}, u32[]{:S(2)}, u32[]{:S(2)}) collective-permute-start(f32[16,2,768]{2,1,0:T(2,128)S(1)} %get-tuple-element.24), channel_id=1, source_target_pairs={{0,1},{1,2},{2,3},{3,4},{4,5},{5,6},{6,7},{7,8},{8,9},{9,10},{10,1... | collective-permute-start | bytes 294920 | tf_op jit(solution)/shard_map/ppermute | solution.py:19
  46.7 31.0 %all-to-all-start = ((f32[32,1,2432]{2,1,0:T(1,128)}), f32[32,1,2432]{2,1,0:T(1,128)S(1)}, u32[]{:S(2)}, u32[]{:S(2)}) async-start(f32[32,1,2432]{2,1,0:T(1,128)} %pad_maximum_fusion.20), calls=%async_computation | async-start | bytes 622592 | tf_op jit(solution)/shard_map/all_to_all | solution.py:247
  53.8 0.9 copy-start.6
  55.5 1.1 copy-start.3
  77.7 17.1 %copy-start.9 = (f32[16,16,768]{2,1,0:T(8,128)S(1)}, f32[16,16,768]{2,1,0:T(8,128)}, u32[]{:S(2)}) copy-start(f32[16,16,768]{2,1,0:T(8,128)} %param.12) | copy-start | bytes 2359300
  94.8 1.1 copy-start.4
  96.0 0.9 copy-start.7
  96.0 1.0 copy-start.8
  98.2 15.8 %collective-permute-start.8 = (f32[16,2,768]{2,1,0:T(2,128)S(1)}, f32[16,2,768]{2,1,0:T(2,128)S(1)}, u32[]{:S(2)}, u32[]{:S(2)}) collective-permute-start(f32[16,2,768]{2,1,0:T(2,128)S(1)} %get-tuple-element.15), channel_id=1, source_target_pairs={{0,1},{1,2},{2,3},{3,4},{4,5},{5,6},{6,7},{7,8},{8,9},{9,10},{10,1... | collective-permute-start | bytes 294920 | tf_op jit(solution)/shard_map/ppermute | solution.py:43
  100.2 13.7 %collective-permute-start.7 = (f32[16,2,768]{2,1,0:T(2,128)S(1)}, f32[16,2,768]{2,1,0:T(2,128)S(1)}, u32[]{:S(2)}, u32[]{:S(2)}) collective-permute-start(f32[16,2,768]{2,1,0:T(2,128)S(1)} %get-tuple-element.16), channel_id=1, source_target_pairs={{1,0},{2,1},{3,2},{4,3},{5,4},{6,5},{7,6},{8,7},{9,8},{10,9},{11,1... | collective-permute-start | bytes 294920 | tf_op jit(solution)/shard_map/ppermute | solution.py:46
  108.0 6.0 %collective-permute-start.6 = (f32[16,1,768]{2,1,0:T(1,128)S(1)}, f32[16,1,768]{2,1,0:T(1,128)S(1)}, u32[]{:S(2)}, u32[]{:S(2)}) collective-permute-start(f32[16,1,768]{2,1,0:T(1,128)S(1)} %get-tuple-element.13), channel_id=1, source_target_pairs={{1,0},{2,1},{3,2},{4,3},{5,4},{6,5},{7,6},{8,7},{9,8},{10,9},{11,1... | collective-permute-start | bytes 147464 | tf_op jit(solution)/shard_map/ppermute | solution.py:20
  116.2 10.2 %collective-permute-start.10 = (f32[16,2,768]{2,1,0:T(2,128)S(1)}, f32[16,2,768]{2,1,0:T(2,128)S(1)}, u32[]{:S(2)}, u32[]{:S(2)}) collective-permute-start(f32[16,2,768]{2,1,0:T(2,128)S(1)} %get-tuple-element.9), channel_id=1, source_target_pairs={{0,1},{1,2},{2,3},{3,4},{4,5},{5,6},{6,7},{7,8},{8,9},{9,10},{10,1... | collective-permute-start | bytes 294920 | tf_op jit(solution)/shard_map/ppermute | solution.py:43
  118.1 10.1 %collective-permute-start.9 = (f32[16,2,768]{2,1,0:T(2,128)S(1)}, f32[16,2,768]{2,1,0:T(2,128)S(1)}, u32[]{:S(2)}, u32[]{:S(2)}) collective-permute-start(f32[16,2,768]{2,1,0:T(2,128)S(1)} %get-tuple-element.10), channel_id=1, source_target_pairs={{1,0},{2,1},{3,2},{4,3},{5,4},{6,5},{7,6},{8,7},{9,8},{10,9},{11,1... | collective-permute-start | bytes 294920 | tf_op jit(solution)/shard_map/ppermute | solution.py:46

commit v2 on v1

v2 whole, which is shorter than its diff:
```python
import jax
import jax.numpy as jnp
from jax import lax
from jax.experimental import pallas as pl
from jax.experimental.pallas import tpu as pltpu
from jax.sharding import PartitionSpec as P


RING = ("group", "tile")
SLOT_ROWS = 1536
UNROLL = 4


def shifted(block, distance):
    total = lax.axis_size(RING)
    return lax.ppermute(block, RING, [(i, (i + distance) % total) for i in range(total)])


def flux_y(v, courant):
    width, axis = v.shape[-1], v.ndim - 1
    ahead, behind = pltpu.roll(v, width - 1, axis), pltpu.roll(v, 1, axis)
    f = courant * (2.0 * ahead + 5.0 * v - behind) * (1.0 / 6.0)
    return v + pltpu.roll(f, 1, axis) - f


def sweep_y(a, courant):
    width, axis = a.shape[-1], a.ndim - 1
    g = courant * (pltpu.roll(a, width - 1, axis) - a)
    return a + (2.0 * pltpu.roll(g, 1, axis) + 5.0 * g - pltpu.roll(g, width - 1, axis)) * (1.0 / 6.0)


def mix_rows(c, mixing):
    levels = c.shape[0]
    f = mixing * (pltpu.roll(c, levels - 1, 0) - c)
    return c + f - pltpu.roll(f, 1, 0)


def mixing_row(mixing, x):
    row = mixing[:, x, :]
    return jnp.concatenate([row, jnp.zeros((1, row.shape[1]), row.dtype)], axis=0)


def sounding_kernel(
    table,
    box,
    far_adjoint,
    far_courant_x,
    far_courant_y,
    far_mixing,
    forcing_0,
    swept_1,
    to_low,
    to_high,
    courant_x,
    courant_y,
    mixing,
    adjoint_in,
    field_done,
    forcing_1,
    row_wide,
    row_ref,
    row_done,
    taken_0,
    taken_1,
    spread_0,
    spread_1,
    *sums,
):
    tiles = box.shape[0]
    width_y = adjoint_in.shape[2]

    def rows_of(t, carry):
        column = box[t, :, 17 * 128 : 18 * 128].astype(jnp.int32)
        step = box[t, :, 18 * 128 :].astype(jnp.int32)
        row = step * SLOT_ROWS + column // (8 * width_y) * width_y + column % width_y
        row_wide[pl.ds(t, 1), :] = row
        return carry

    lax.fori_loop(0, tiles, rows_of, 0, unroll=8)
    copy_rows = pltpu.make_async_copy(row_wide, row_ref, row_done)
    copy_rows.start()
    pairs = (
        (far_adjoint, adjoint_in),
        (far_courant_x, courant_x),
        (far_courant_y, courant_y),
        (far_mixing, mixing),
    )
    copies = [pltpu.make_async_copy(*pair, field_done.at[n]) for n, pair in enumerate(pairs)]
    for copy in copies:
        copy.start()

    def clear(i, carry):
        for acc in sums:
            acc[pl.ds(pl.multiple_of(i * 128, 128), 128), :] = jnp.zeros((128, 128), jnp.float32)
        return carry

    lax.fori_loop(0, 24, clear, 0)
    copy_rows.wait()

    sub = lax.broadcasted_iota(jnp.int32, (8, 128), 0)

    def gather(t, taken):
        for k in range(128):
            taken[k : k + 1, :] = table[pl.ds(row_ref[t, k], 1), :]

    def observe(t, taken, spread):
        cells = taken[...].T
        rows = [box[t, :, f * 128 : f * 128 + 128] for f in range(18)]
        total = cells[0:8, :] * rows[0]
        for level in range(1, 16):
            total = total + cells[level * 8 : level * 8 + 8, :] * rows[level]
        own = sub == (rows[17].astype(jnp.int32) // 768) % 8
        observed = jnp.sum(jnp.where(own, total, 0.0), axis=0, keepdims=True)
        misfit = jnp.where(own, jnp.broadcast_to(observed - rows[16], (8, 128)), 0.0)
        spread[...] = jnp.concatenate([misfit * rows[level] for level in range(16)], axis=0).T

    def scatter(t, spread):
        for k in range(128):
            acc = sums[k % len(sums)]
            at = pl.ds(row_ref[t, k], 1)
            acc[at, :] = acc[at, :] + spread[k : k + 1, :]

    spread_1[...] = jnp.zeros((128, 128), jnp.float32)
    gather(0, taken_0)

    def two(i, carry):
        t = 2 * i
        observe(t, taken_0, spread_0)
        gather(t + 1, taken_1)
        scatter(jnp.maximum(t - 1, 0), spread_1)
        observe(t + 1, taken_1, spread_1)
        gather(jnp.minimum(t + 2, tiles - 1), taken_0)
        scatter(t, spread_0)
        return carry

    lax.fori_loop(0, tiles // 2, two, 0)
    scatter(tiles - 1, spread_1)

    def back(i, carry):
        off = pl.multiple_of(i * 128, 128)
        for s, ref in enumerate((forcing_0, forcing_1)):
            for h in range(2):
                at = pl.ds(pl.multiple_of(s * SLOT_ROWS + h * 768 + off, 128), 128)
                block = sums[0][at, :]
                for acc in sums[1:]:
                    block = block + acc[at, :]
                ref[:, h * 8 : h * 8 + 8, pl.ds(off, 128)] = block.T.reshape(16, 8, 128)
        return carry

    lax.fori_loop(0, 6, back, 0)
    levels = adjoint_in.shape[0]
    for copy in copies:
        copy.wait()

    def first_step(level, carry):
        here, below = carry
        above = jnp.minimum(level + 1, levels - 1)
        upper = adjoint_in[above] + forcing_1[above]
        flux = mixing[jnp.minimum(level, levels - 2)] * (upper - here)
        flux = jnp.where(level < levels - 1, flux, 0.0)
        swept_1[level] = sweep_y(here + flux - below, courant_y[level])
        return upper, flux

    start = adjoint_in[0] + forcing_1[0]
    lax.fori_loop(0, levels, first_step, (start, jnp.zeros_like(start)), unroll=UNROLL)
    b = {x: swept_1[:, x, :] for x in (0, 1, 2, 3, 14, 15)}
    g = {x: courant_x[:, x, :] * (b[x + 1] - b[x]) for x in (0, 1, 2, 14)}
    to_low[0] = b[0]
    to_low[1] = g[0]
    to_low[2] = b[0] + (5.0 * g[0] - g[1]) * (1.0 / 6.0) + forcing_0[:, 0, :]
    a = b[1] + (2.0 * g[0] + 5.0 * g[1] - g[2]) * (1.0 / 6.0) + forcing_0[:, 1, :]
    to_low[3] = sweep_y(mix_rows(a, mixing_row(mixing, 1)), courant_y[:, 1, :])
    to_high[0] = b[15]
    to_high[1] = b[15] + g[14] * (1.0 / 3.0) + forcing_0[:, 15, :]


def adjoint_to_edges(table, box, adjoint_in, *winds):
    vmem, hbm = (pl.BlockSpec(memory_space=space) for space in (pltpu.VMEM, pltpu.HBM))
    levels, _, width_y = adjoint_in.shape
    edges = tuple(jax.ShapeDtypeStruct((n, levels, width_y), jnp.float32) for n in (4, 2))
    return pl.pallas_call(
        sounding_kernel,
        out_shape=shapes_of(adjoint_in, adjoint_in) + edges + shapes_of(*winds),
        in_specs=[vmem] * 2 + [hbm] * 4,
        out_specs=(vmem,) * 7,
        scratch_shapes=[
            pltpu.VMEM(adjoint_in.shape, jnp.float32),
            pltpu.SemaphoreType.DMA((4,)),
            pltpu.VMEM(adjoint_in.shape, jnp.float32),
            pltpu.VMEM((box.shape[0], 128), jnp.int32),
            pltpu.SMEM((box.shape[0], 128), jnp.int32),
            pltpu.SemaphoreType.DMA,
        ]
        + [pltpu.VMEM((128, 128), jnp.float32)] * 4
        + [pltpu.VMEM((2 * SLOT_ROWS, 128), jnp.float32)] * 8,
        compiler_params=pltpu.CompilerParams(vmem_limit_bytes=26 * 2**20),
    )(table, box, adjoint_in, *winds)


def final_kernel(
    swept_1, forcing_0, courant_x, courant_y, mixing, low, high, rim_low, rim_high, out, edges
):
    levels, width_x = swept_1.shape[:2]
    wind_low, wind_high = rim_low.at[4:7], rim_high.at[2:5]
    sixth = 1.0 / 6.0
    b_first, b_next, b_last = swept_1[:, 0, :], swept_1[:, 1, :], swept_1[:, width_x - 1, :]
    g_low = wind_low[0] * (b_first - low[0])
    g_first = courant_x[:, 0, :] * (b_next - b_first)
    g_last = courant_x[:, width_x - 1, :] * (high[0] - b_last)
    before = sweep_y(mix_rows(low[1] + (5.0 * g_low - g_first) * sixth, wind_low[2]), wind_low[1])
    after = sweep_y(mix_rows(high[2] + g_last * (1.0 / 3.0), wind_high[2]), wind_high[1])
    edges[0] = g_low
    edges[1] = before
    edges[2] = after
    edges[3] = wind_high[0] * (high[3] - after)
    sub = lax.broadcasted_iota(jnp.int32, swept_1.shape[1:], 0)

    def up(field, row):
        return jnp.where(sub == width_x - 1, row, pltpu.roll(field, width_x - 1, 0))

    def down(field, row):
        return jnp.where(sub == 0, row, pltpu.roll(field, 1, 0))

    def sweep_x(field, courant, after_last, g_before, g_after):
        g = courant * (up(field, after_last) - field)
        return field + (2.0 * down(g, g_before) + 5.0 * g - up(g, g_after)) * sixth

    def entering(level):
        at = pl.ds(level, 1)
        swept = sweep_x(
            swept_1[level], courant_x[level], high[0, at, :], edges[0, at, :], high[1, at, :]
        )
        return swept + forcing_0[level]

    def second_step(level, carry):
        here, below = carry
        at = pl.ds(level, 1)
        upper = entering(jnp.minimum(level + 1, levels - 1))
        flux = mixing[jnp.minimum(level, levels - 2)] * (upper - here)
        flux = jnp.where(level < levels - 1, flux, 0.0)
        b = sweep_y(here + flux - below, courant_y[level])
        c = courant_x[level]
        g_before = wind_low[0, at, :] * (b[0:1, :] - edges[1, at, :])
        out[level] = sweep_x(b, c, edges[2, at, :], g_before, edges[3, at, :])
        return upper, flux

    start = entering(0)
    lax.fori_loop(0, levels, second_step, (start, jnp.zeros_like(start)), unroll=UNROLL)


def adjoint_final(*fields):
    vmem = pl.BlockSpec(memory_space=pltpu.VMEM)
    shape = fields[0].shape
    return pl.pallas_call(
        final_kernel,
        out_shape=jax.ShapeDtypeStruct(shape, jnp.float32),
        in_specs=[vmem] * len(fields),
        out_specs=vmem,
        scratch_shapes=[pltpu.VMEM((4, shape[0], shape[2]), jnp.float32)],
        compiler_params=pltpu.CompilerParams(vmem_limit_bytes=4 * 2**20),
    )(*fields)


def pack_soundings(snd_column, snd_count, snd_step, snd_value, snd_weight, snd_kernel):
    _, tile_count, _ = snd_column.shape
    position = lax.broadcasted_iota(jnp.int32, snd_column.shape, 2)
    weight = jnp.where(position < snd_count[:, :, None], snd_weight, jnp.zeros_like(snd_weight))
    root = jnp.sqrt(weight)
    parts = (
        snd_kernel * root[:, :, None, :],
        snd_value * root,
        snd_column.astype(jnp.float32),
        snd_step.astype(jnp.float32),
    )
    return jnp.concatenate([p.reshape(tile_count, 1, -1) for p in parts], axis=2)


def rim_kernel(*refs):
    sources, (to_high, to_low), local, done = refs[:3], refs[4:6], refs[6:9], refs[9]
    tracer = refs[3]
    copies = [
        pltpu.make_async_copy(source, target, done.at[n])
        for n, (source, target) in enumerate(zip(sources, local))
    ]
    for copy in copies:
        copy.start()
    for copy in copies:
        copy.wait()
    courant_x, courant_y, mixing = local
    last = tracer.shape[1] - 1
    sixth = 1.0 / 6.0
    c = {x: tracer[:, x, :] for x in (0, 1, last - 3, last - 2, last - 1, last)}
    w = {x: courant_x[:, x, :] for x in (0, last - 2, last - 1, last)}

    def flux(x):
        return w[x] * (2.0 * c[x + 1] + 5.0 * c[x] - c[x - 1]) * sixth

    inner = flux(last - 1)
    swept = flux_y(c[last - 1] + flux(last - 2) - inner, courant_y[:, last - 1, :])
    to_high[0] = mix_rows(swept, mixing_row(mixing, last - 1))
    known = w[last] * (5.0 * c[last] - c[last - 1]) * sixth
    to_high[1] = c[last] + inner - known
    to_high[2] = known
    to_high[3] = c[last]
    to_low[0] = c[0]
    to_low[1] = c[0] - w[0] * (2.0 * c[1] + 5.0 * c[0]) * sixth
    for ref, first, x in ((to_high, 4, last), (to_low, 2, 0)):
        ref[first] = courant_x[:, x, :]
        ref[first + 1] = courant_y[:, x, :]
        ref[first + 2] = mixing_row(mixing, x)


def shapes_of(*fields):
    return tuple(jax.ShapeDtypeStruct(x.shape, x.dtype) for x in fields)


def rims(tracer, *winds):
    vmem = pl.BlockSpec(memory_space=pltpu.VMEM)
    levels, _, width_y = tracer.shape
    edges = tuple(jax.ShapeDtypeStruct((n, levels, width_y), jnp.float32) for n in (7, 5))
    return pl.pallas_call(
        rim_kernel,
        out_shape=edges + shapes_of(*winds),
        in_specs=[pl.BlockSpec(memory_space=pltpu.HBM)] * len(winds) + [vmem],
        out_specs=(vmem,) * 5,
        scratch_shapes=[pltpu.SemaphoreType.DMA((len(winds),))],
        compiler_params=pltpu.CompilerParams(vmem_limit_bytes=8 * 2**20),
    )(*winds, tracer)


def forward_kernel(tracer, low, high, courant_x, courant_y, mixing, table, first, second, edges):
    levels, width_x, width_y = tracer.shape
    sixth = 1.0 / 6.0
    last = width_x - 1
    sub = lax.broadcasted_iota(jnp.int32, tracer.shape[1:], 0)
    wind_low, wind_high = low[4], high[2]
    c_first, c_last = tracer[:, 0, :], tracer[:, last, :]
    reach = wind_low * c_first * (1.0 / 3.0)
    edges[0] = low[3]
    edges[1] = low[2] + reach
    edges[2] = high[0]
    near = mix_rows(flux_y(low[1] - reach, low[5]), low[6])
    flux_last = (
        courant_x[:, last, :] * (2.0 * high[0] + 5.0 * c_last - tracer[:, last - 1, :]) * sixth
    )
    after = flux_y(high[1] + wind_high * c_last * sixth + flux_last, high[3])
    edges[3] = near
    edges[5] = mix_rows(after, high[4])

    def step(source, target, e):
        def entering(level):
            at = pl.ds(level, 1)
            c, w = source[level], courant_x[level]
            ahead = jnp.where(sub == last, edges[e + 2, at, :], pltpu.roll(c, last, 0))
            behind = jnp.where(sub == 0, edges[e, at, :], pltpu.roll(c, 1, 0))
            f = w * (2.0 * ahead + 5.0 * c - behind) * sixth
            swept = c + jnp.where(sub == 0, edges[e + 1, at, :], pltpu.roll(f, 1, 0)) - f
            return flux_y(swept, courant_y[level])

        def one(level, carry):
            here, below = carry
            upper = entering(jnp.minimum(level + 1, levels - 1))
            flux = mixing[jnp.minimum(level, levels - 2)] * (upper - here)
            flux = jnp.where(level < levels - 1, flux, 0.0)
            target[level] = here + flux - below
            return upper, flux

        start = entering(0)
        lax.fori_loop(0, levels, one, (start, jnp.zeros_like(start)), unroll=UNROLL)

    step(tracer, first, 0)
    edges[4] = wind_low * (2.0 * first[:, 0, :] + 5.0 * near - low[0]) * sixth
    step(first, second, 3)

    def to_rows(i, carry):
        off = pl.multiple_of(i * 128, 128)
        for s, ref in enumerate((first, second)):
            for h in range(2):
                block = ref[:, h * 8 : h * 8 + 8, pl.ds(off, 128)].reshape(128, 128)
                at = pl.multiple_of(s * SLOT_ROWS + h * width_y + off, 128)
                table[pl.ds(at, 128), :] = block.T
        return carry

    lax.fori_loop(0, width_y // 128, to_rows, 0)


def forward(*fields):
    vmem = pl.BlockSpec(memory_space=pltpu.VMEM)
    shape = fields[0].shape
    return pl.pallas_call(
        forward_kernel,
        out_shape=jax.ShapeDtypeStruct((2 * SLOT_ROWS, 128), jnp.float32),
        in_specs=[vmem] * len(fields),
        out_specs=vmem,
        scratch_shapes=[pltpu.VMEM(shape, jnp.float32)] * 2
        + [pltpu.VMEM((6, shape[0], shape[2]), jnp.float32)],
        compiler_params=pltpu.CompilerParams(vmem_limit_bytes=6 * 2**20),
    )(*fields)


def program(
    checkpoint,
    adjoint_in,
    courant_x,
    courant_y,
    mixing,
    snd_column,
    snd_count,
    snd_step,
    snd_value,
    snd_weight,
    snd_kernel,
):
    tiles = snd_column.shape[1]
    *winds, adjoint_in = (
        pltpu.with_memory_space_constraint(x, pltpu.HBM)
        for x in (courant_x, courant_y, mixing, adjoint_in)
    )
    tracer = shifted(checkpoint, tiles)
    packed = pack_soundings(
        snd_column, snd_count, snd_step, snd_value, snd_weight, snd_kernel
    )
    box = lax.all_to_all(packed, "tile", split_axis=0, concat_axis=0, tiled=True)
    to_high, to_low, *near_winds = rims(tracer, *winds)
    low = shifted(to_high, 1)
    high = shifted(to_low, -1)
    table = forward(tracer, low, high, *near_winds)
    forcing_0, swept_1, to_low, to_high, *near_winds = adjoint_to_edges(
        table, box, adjoint_in, *winds
    )
    from_high = shifted(to_low, -1)
    from_low = shifted(to_high, 1)
    return adjoint_final(
        swept_1, forcing_0, *near_winds, from_low, from_high, low, high
    )


def solution(mesh):
    return jax.shard_map(
        program,
        mesh=mesh,
        in_specs=(P(None, RING, None),) * 5
        + (P(RING, None, None), P(RING, None))
        + (P(RING, None, None),) * 3
        + (P(RING, None, None, None),),
        out_specs=P(None, RING, None),
        check_vma=False,
    )
```

time: 130 us -> 93.3 us (0.72)
  starting transfers between devices: 53.1 us -> 38.3 us
  waiting for transfers between devices: 40.8 us -> 29.3 us
  other arithmetic: 11.9 us -> 4.31 us
  local copies, waits for them, and re-layouts: 6.49 us -> 0.01 us
  Pallas kernels: 17 us -> 20.5 us
    ppermute x11 -> x5, starting transfers between devices: 46.9 us -> 20.4 us  [shifted(): lax.ppermute(block, RING, [(i, (i + distance) % total) for i in range(tot...]
    all_to_all x1, waiting for transfers between devices: 20.9 us -> 0.01 us  [program(): lax.all_to_all(packed, 'tile', split_axis=0, concat_axis=0, tiled=True)]
    all_to_all x1, starting transfers between devices: 6.24 us -> 17.9 us  [program(): lax.all_to_all(packed, 'tile', split_axis=0, concat_axis=0, tiled=True)]
    ppermute x11 -> x5, waiting for transfers between devices: 19.9 us -> 29.3 us  [shifted(): lax.ppermute(block, RING, [(i, (i + distance) % total) for i in range(tot...]
    unnamed x25 -> x2, local copies, waits for them, and re-layouts: 3.98 us -> 0.01 us
    pallas_call x1 -> x4, Pallas kernels: 17 us -> 20.5 us  [the longest x1 11.4 us: adjoint_to_edges(): pl.pallas_call(sounding_kernel, out_shape=shapes_of(adjoint_in, adjoint_i...]
    div x4 -> x0, other arithmetic: 2.75 us -> none  [sweep_forward(): courant_face * (2.0 * piece_of(2, interior + 3) + 5.0 * piece_of(1, inter...]
    slice x10 -> x0, local copies, waits for them, and re-layouts: 2.51 us -> none  [the longest x3 1.32 us: padded_2(): initial = lax.slice_in_dim(x, 0, width, axis=dim)]
  transfers between devices with their start and end apart: 12 -> 6, of which waited for: 7 -> 4; matrix products, arithmetic and copies ran while one was open for 5% -> 0% of each run, Pallas kernels for 0% -> 7%
where the time goes in v2:
time: 93.3 us; the launch traced here: 92.5 us
  starting transfers between devices  38.3 us (41%)
  waiting for transfers between devices  29.3 us (31%)
  Pallas kernels  20.5 us (22%)
  other arithmetic  4.31 us (5%)
    ppermute x5, waiting for transfers between devices, shifted(): lax.ppermute(block, RING, [(i, (i + distance) % total) for i in range(tot...  29.3 us
    ppermute x5, starting transfers between devices, shifted(): lax.ppermute(block, RING, [(i, (i + distance) % total) for i in range(tot...  20.4 us
    all_to_all x1, starting transfers between devices, program(): lax.all_to_all(packed, 'tile', split_axis=0, concat_axis=0, tiled=True)  17.9 us
    pallas_call x1, Pallas kernels, adjoint_to_edges(): pl.pallas_call(sounding_kernel, out_shape=shapes_of(adjoint_in, adjoint_i...  11.4 us
    pallas_call x1, Pallas kernels, forward(): pl.pallas_call(forward_kernel, out_shape=jax.ShapeDtypeStruct((2 * SLOT_R...  4.09 us
    pallas_call x1, Pallas kernels, adjoint_final(): pl.pallas_call(final_kernel, out_shape=jax.ShapeDtypeStruct(shape, jnp.fl...  2.94 us
    pallas_call x1, Pallas kernels, rims(): pl.pallas_call(rim_kernel, out_shape=edges + shapes_of(*winds), in_specs=...  2.09 us
  transfers between devices with their start and end apart: 6, of which 4 were waited for; matrix products, arithmetic and copies ran while one was open for 0% of the time, Pallas kernels for 7%

profile of v2, /device:TPU:24, one launch (start us, length us, event | category | flops | bytes accessed | tf_op | source)
XLA Modules:
  0.0 92.5 jit_solution(4216019893034169600)
XLA Ops:
  0.0 0.0 copy-start
  0.0 0.8 convert_element_type.6
  0.8 0.7 convert_element_type.7
  1.5 0.8 fusion.1
  2.3 1.0 %broadcast_multiply_fusion = f32[1,32,16,128]{3,2,1,0:T(8,128)S(1)} fusion(f32[1,32,16,128]{3,2,1,0:T(8,128)} %param.21, f32[32,128]{1,0:T(8,128)S(1)} %get-tuple-element.29), kind=kLoop, calls=%fused_computation.1 | loop fusion | flops 65536 | bytes 540672 | tf_op jit(solution)/shard_map/mul | solution.py:270
  3.3 1.0 %pad_maximum_fusion = f32[32,1,2432]{2,1,0:T(1,128)} fusion(f32[32,1,128]{2,1,0:T(1,128)S(1)} %bitcast.9, f32[32,1,128]{2,1,0:T(1,128)S(1)} %bitcast.8, f32[32,1,128]{2,1,0:T(1,128)S(1)} %bitcast.10, f32[32,1,2048]{2,1,0:T(1,128)S(1)} %bitcast.7), kind=kLoop, calls=%fused_computation | loop fusion | flops 233472 | bytes 622592 | tf_op jit(solution)/shard_map/concatenate | solution.py:275
  4.3 17.9 %all-to-all-start = ((f32[32,1,2432]{2,1,0:T(1,128)}), f32[32,1,2432]{2,1,0:T(1,128)S(1)}, u32[]{:S(2)}, u32[]{:S(2)}) async-start(f32[32,1,2432]{2,1,0:T(1,128)} %pad_maximum_fusion), calls=%async_computation | async-start | bytes 622592 | tf_op jit(solution)/shard_map/all_to_all | solution.py:423
  22.3 0.0 copy-done
  22.3 1.9 %collective-permute-start = (f32[16,16,768]{2,1,0:T(8,128)S(1)}, f32[16,16,768]{2,1,0:T(8,128)S(1)}, u32[]{:S(2)}, u32[]{:S(2)}) collective-permute-start(f32[16,16,768]{2,1,0:T(8,128)S(1)} %copy-done), channel_id=1, source_target_pairs={{0,32},{1,33},{2,34},{3,35},{4,36},{5,37},{6,38},{7,39},{8,40},{9,... | collective-permute-start | bytes 2359304 | tf_op jit(solution)/shard_map/ppermute | solution.py:16
  24.2 14.4 %collective-permute-done.refs_3_.tracer = f32[16,16,768]{2,1,0:T(8,128)S(1)} collective-permute-done((f32[16,16,768]{2,1,0:T(8,128)S(1)}, f32[16,16,768]{2,1,0:T(8,128)S(1)}, u32[]{:S(2)}, u32[]{:S(2)}) %collective-permute-start) | collective-permute-done | bytes 786464 | tf_op jit(solution)/shard_map/ppermute | solution.py:16
  38.6 2.1 %shard_map.112 = (f32[7,16,768]{2,1,0:T(8,128)S(1)}, f32[5,16,768]{2,1,0:T(8,128)S(1)}, f32[16,16,768]{2,1,0:T(8,128)S(1)}, f32[16,16,768]{2,1,0:T(8,128)S(1)}, f32[15,16,768]{2,1,0:T(8,128)S(1)}) custom-call(f32[16,16,768]{2,1,0:T(8,128)} %far_courant_x.1, f32[16,16,768]{2,1,0:T(8,128)} %far_courant_y.1, f32[15,16,768]{2,1,0:T(8,128)} %far_mixing.1, ...), custom_call_target="tpu_custom_call" | custom-call | tf_op jit(solution)/shard_map/pallas_call | solution.py:321
  40.7 3.7 %collective-permute-start.1 = (f32[7,16,768]{2,1,0:T(8,128)S(1)}, f32[7,16,768]{2,1,0:T(8,128)S(1)}, u32[]{:S(2)}, u32[]{:S(2)}) collective-permute-start(f32[7,16,768]{2,1,0:T(8,128)S(1)} %get-tuple-element.17), channel_id=1, source_target_pairs={{0,1},{1,2},{2,3},{3,4},{4,5},{5,6},{6,7},{7,8},{8,9},{9,10},{10,1... | collective-permute-start | bytes 1032200 | tf_op jit(solution)/shard_map/ppermute | solution.py:16
  44.4 6.1 %collective-permute-start.2 = (f32[5,16,768]{2,1,0:T(8,128)S(1)}, f32[5,16,768]{2,1,0:T(8,128)S(1)}, u32[]{:S(2)}, u32[]{:S(2)}) collective-permute-start(f32[5,16,768]{2,1,0:T(8,128)S(1)} %get-tuple-element.18), channel_id=1, source_target_pairs={{0,511},{1,0},{2,1},{3,2},{4,3},{5,4},{6,5},{7,6},{8,7},{9,8},{10,... | collective-permute-start | bytes 737288 | tf_op jit(solution)/shard_map/ppermute | solution.py:16
  50.5 5.3 %collective-permute-done.2.high.rim_high = f32[5,16,768]{2,1,0:T(8,128)S(1)} collective-permute-done((f32[5,16,768]{2,1,0:T(8,128)S(1)}, f32[5,16,768]{2,1,0:T(8,128)S(1)}, u32[]{:S(2)}, u32[]{:S(2)}) %collective-permute-start.2) | collective-permute-done | bytes 245792 | tf_op jit(solution)/shard_map/ppermute | solution.py:16
  55.8 1.4 %collective-permute-done.1.low.rim_low = f32[7,16,768]{2,1,0:T(8,128)S(1)} collective-permute-done((f32[7,16,768]{2,1,0:T(8,128)S(1)}, f32[7,16,768]{2,1,0:T(8,128)S(1)}, u32[]{:S(2)}, u32[]{:S(2)}) %collective-permute-start.1) | collective-permute-done | bytes 344096 | tf_op jit(solution)/shard_map/ppermute | solution.py:16
  57.2 4.1 %shard_map.113.table = f32[3072,128]{1,0:T(8,128)S(1)} custom-call(f32[16,16,768]{2,1,0:T(8,128)S(1)} %collective-permute-done.refs_3_.tracer, f32[7,16,768]{2,1,0:T(8,128)S(1)} %collective-permute-done.1.low.rim_low, f32[5,16,768]{2,1,0:T(8,128)S(1)} %collective-permute-done.2.high.rim_high, f32[16,16,768]{2,1,0:T(8,128)S(1)} %get-tuple-element.19.courant_x, ...), custom_call_target="tpu_custom_call" | custom-call | tf_op jit(solution)/shard_map/pallas_call | solution.py:390
  61.3 0.0 all-to-all-done.box
  61.3 11.4 %shard_map.114 = (f32[16,16,768]{2,1,0:T(8,128)S(1)}, f32[16,16,768]{2,1,0:T(8,128)S(1)}, f32[4,16,768]{2,1,0:T(8,128)S(1)}, f32[2,16,768]{2,1,0:T(8,128)S(1)}, ...) custom-call(f32[3072,128]{1,0:T(8,128)S(1)} %shard_map.113.table, ...), custom_call_target="tpu_custom_call" | custom-call | tf_op jit(solution)/shard_map/pallas_call | solution.py:181
  72.7 6.7 %collective-permute-start.4 = (f32[4,16,768]{2,1,0:T(8,128)S(1)}, f32[4,16,768]{2,1,0:T(8,128)S(1)}, u32[]{:S(2)}, u32[]{:S(2)}) collective-permute-start(f32[4,16,768]{2,1,0:T(8,128)S(1)} %get-tuple-element.28), channel_id=1, source_target_pairs={{0,511},{1,0},{2,1},{3,2},{4,3},{5,4},{6,5},{7,6},{8,7},{9,8},{10,... | collective-permute-start | bytes 589832 | tf_op jit(solution)/shard_map/ppermute | solution.py:16
  79.4 1.9 %collective-permute-start.3 = (f32[2,16,768]{2,1,0:T(8,128)S(1)}, f32[2,16,768]{2,1,0:T(8,128)S(1)}, u32[]{:S(2)}, u32[]{:S(2)}) collective-permute-start(f32[2,16,768]{2,1,0:T(8,128)S(1)} %get-tuple-element.27), channel_id=1, source_target_pairs={{0,1},{1,2},{2,3},{3,4},{4,5},{5,6},{6,7},{7,8},{8,9},{9,10},{10,1... | collective-permute-start | bytes 294920 | tf_op jit(solution)/shard_map/ppermute | solution.py:16
  81.3 8.2 %collective-permute-done.3.low = f32[2,16,768]{2,1,0:T(8,128)S(1)} collective-permute-done((f32[2,16,768]{2,1,0:T(8,128)S(1)}, f32[2,16,768]{2,1,0:T(8,128)S(1)}, u32[]{:S(2)}, u32[]{:S(2)}) %collective-permute-start.3) | collective-permute-done | bytes 98336 | tf_op jit(solution)/shard_map/ppermute | solution.py:16
  89.6 0.0 collective-permute-done.4.high
  89.6 2.9 %shard_map.115 = f32[16,16,768]{2,1,0:T(8,128)} custom-call(f32[16,16,768]{2,1,0:T(8,128)S(1)} %get-tuple-element.22.swept_1, f32[16,16,768]{2,1,0:T(8,128)S(1)} %get-tuple-element.23.forcing_0, f32[16,16,768]{2,1,0:T(8,128)S(1)} %get-tuple-element.24.courant_x, f32[16,16,768]{2,1,0:T(8,128)S(1)} %get-tuple-element.25.courant_y, ...), custom_call_target="tpu_custom_call" | custom-call | tf_op jit(solution)/shard_map/pallas_call | solution.py:254
Async XLA Ops:
  0.0 22.3 %copy-start = (f32[16,16,768]{2,1,0:T(8,128)S(1)}, f32[16,16,768]{2,1,0:T(8,128)}, u32[]{:S(2)}) copy-start(f32[16,16,768]{2,1,0:T(8,128)} %param.11) | copy-start | bytes 2359300
  4.3 57.0 %all-to-all-start = ((f32[32,1,2432]{2,1,0:T(1,128)}), f32[32,1,2432]{2,1,0:T(1,128)S(1)}, u32[]{:S(2)}, u32[]{:S(2)}) async-start(f32[32,1,2432]{2,1,0:T(1,128)} %pad_maximum_fusion), calls=%async_computation | async-start | bytes 622592 | tf_op jit(solution)/shard_map/all_to_all | solution.py:423
  22.3 16.3 %collective-permute-start = (f32[16,16,768]{2,1,0:T(8,128)S(1)}, f32[16,16,768]{2,1,0:T(8,128)S(1)}, u32[]{:S(2)}, u32[]{:S(2)}) collective-permute-start(f32[16,16,768]{2,1,0:T(8,128)S(1)} %copy-done), channel_id=1, source_target_pairs={{0,32},{1,33},{2,34},{3,35},{4,36},{5,37},{6,38},{7,39},{8,40},{9,... | collective-permute-start | bytes 2359304 | tf_op jit(solution)/shard_map/ppermute | solution.py:16
  40.7 16.5 %collective-permute-start.1 = (f32[7,16,768]{2,1,0:T(8,128)S(1)}, f32[7,16,768]{2,1,0:T(8,128)S(1)}, u32[]{:S(2)}, u32[]{:S(2)}) collective-permute-start(f32[7,16,768]{2,1,0:T(8,128)S(1)} %get-tuple-element.17), channel_id=1, source_target_pairs={{0,1},{1,2},{2,3},{3,4},{4,5},{5,6},{6,7},{7,8},{8,9},{9,10},{10,1... | collective-permute-start | bytes 1032200 | tf_op jit(solution)/shard_map/ppermute | solution.py:16
  44.4 11.4 %collective-permute-start.2 = (f32[5,16,768]{2,1,0:T(8,128)S(1)}, f32[5,16,768]{2,1,0:T(8,128)S(1)}, u32[]{:S(2)}, u32[]{:S(2)}) collective-permute-start(f32[5,16,768]{2,1,0:T(8,128)S(1)} %get-tuple-element.18), channel_id=1, source_target_pairs={{0,511},{1,0},{2,1},{3,2},{4,3},{5,4},{6,5},{7,6},{8,7},{9,8},{10,... | collective-permute-start | bytes 737288 | tf_op jit(solution)/shard_map/ppermute | solution.py:16
  72.7 16.9 %collective-permute-start.4 = (f32[4,16,768]{2,1,0:T(8,128)S(1)}, f32[4,16,768]{2,1,0:T(8,128)S(1)}, u32[]{:S(2)}, u32[]{:S(2)}) collective-permute-start(f32[4,16,768]{2,1,0:T(8,128)S(1)} %get-tuple-element.28), channel_id=1, source_target_pairs={{0,511},{1,0},{2,1},{3,2},{4,3},{5,4},{6,5},{7,6},{8,7},{9,8},{10,... | collective-permute-start | bytes 589832 | tf_op jit(solution)/shard_map/ppermute | solution.py:16
  79.4 10.2 %collective-permute-start.3 = (f32[2,16,768]{2,1,0:T(8,128)S(1)}, f32[2,16,768]{2,1,0:T(8,128)S(1)}, u32[]{:S(2)}, u32[]{:S(2)}) collective-permute-start(f32[2,16,768]{2,1,0:T(8,128)S(1)} %get-tuple-element.27), channel_id=1, source_target_pairs={{0,1},{1,2},{2,3},{3,4},{4,5},{5,6},{6,7},{7,8},{8,9},{9,10},{10,1... | collective-permute-start | bytes 294920 | tf_op jit(solution)/shard_map/ppermute | solution.py:16

commit v3 on v2

--- a/solution.py
+++ b/solution.py
@@ -261,18 +261,57 @@
     )(*fields)
 
 
-def pack_soundings(snd_column, snd_count, snd_step, snd_value, snd_weight, snd_kernel):
-    _, tile_count, _ = snd_column.shape
-    position = lax.broadcasted_iota(jnp.int32, snd_column.shape, 2)
-    weight = jnp.where(position < snd_count[:, :, None], snd_weight, jnp.zeros_like(snd_weight))
-    root = jnp.sqrt(weight)
-    parts = (
-        snd_kernel * root[:, :, None, :],
-        snd_value * root,
-        snd_column.astype(jnp.float32),
-        snd_step.astype(jnp.float32),
-    )
-    return jnp.concatenate([p.reshape(tile_count, 1, -1) for p in parts], axis=2)
+def pack_kernel(count, *refs):
+    sources, packed, local, root, done = refs[:5], refs[5], refs[6:11], refs[11], refs[12]
+    copies = [
+        pltpu.make_async_copy(source, target, done.at[n])
+        for n, (source, target) in enumerate(zip(sources, local))
+    ]
+    for copy in copies:
+        copy.start()
+    column, step, value, weight, kernel = local
+    tiles, capacity = column.shape[1:]
+    levels = kernel.shape[2]
+    position = lax.broadcasted_iota(jnp.int32, (1, capacity), 1)
+    for copy in copies:
+        copy.wait()
+    for t in range(tiles):
+        root[t : t + 1, :] = jnp.where(position < count[0, t], weight[0, t : t + 1, :], 0.0)
+    root[...] = jnp.sqrt(root[...])
+
+    def one(t, carry):
+        at = pl.ds(t, 1)
+        scale = root[at, :]
+        rows = kernel[0, t] * scale
+        for level in range(levels):
+            packed[t, :, level * capacity : (level + 1) * capacity] = rows[level : level + 1, :]
+        rest = (
+            value[0, at, :] * scale,
+            column[0, at, :].astype(jnp.float32),
+            step[0, at, :].astype(jnp.float32),
+        )
+        for f, part in enumerate(rest, levels):
+            packed[t, :, f * capacity : (f + 1) * capacity] = part
+        return carry
+
+    lax.fori_loop(0, tiles, one, 0, unroll=4)
+
+
+def pack(count, *fields):
+    _, tiles, levels, capacity = fields[4].shape
+    vmem, hbm = (pl.BlockSpec(memory_space=space) for space in (pltpu.VMEM, pltpu.HBM))
+    return pl.pallas_call(
+        pack_kernel,
+        out_shape=jax.ShapeDtypeStruct((tiles, 1, (levels + 3) * capacity), jnp.float32),
+        in_specs=[pl.BlockSpec(memory_space=pltpu.SMEM)] + [hbm] * len(fields),
+        out_specs=vmem,
+        scratch_shapes=[pltpu.VMEM(x.shape, x.dtype) for x in fields]
+        + [
+            pltpu.VMEM((tiles, capacity), jnp.float32),
+            pltpu.SemaphoreType.DMA((len(fields),)),
+        ],
+        compiler_params=pltpu.CompilerParams(vmem_limit_bytes=4 * 2**20),
+    )(count, *fields)
 
 
 def rim_kernel(*refs):
@@ -412,14 +451,12 @@
     snd_kernel,
 ):
     tiles = snd_column.shape[1]
-    *winds, adjoint_in = (
-        pltpu.with_memory_space_constraint(x, pltpu.HBM)
-        for x in (courant_x, courant_y, mixing, adjoint_in)
-    )
+    fields = (snd_count, snd_column, snd_step, snd_value, snd_weight, snd_kernel)
+    fields += (courant_x, courant_y, mixing, adjoint_in)
+    *fields, adjoint_in = (pltpu.with_memory_space_constraint(x, pltpu.HBM) for x in fields)
+    winds = fields[6:]
     tracer = shifted(checkpoint, tiles)
-    packed = pack_soundings(
-        snd_column, snd_count, snd_step, snd_value, snd_weight, snd_kernel
-    )
+    packed = pack(*fields[:6])
     box = lax.all_to_all(packed, "tile", split_axis=0, concat_axis=0, tiled=True)
     to_high, to_low, *near_winds = rims(tracer, *winds)
     low = shifted(to_high, 1)

time: 93.3 us -> 91.7 us (0.983)
  other arithmetic: 4.31 us -> 0 us
  Pallas kernels: 20.5 us -> 23.2 us
    pallas_call x0 -> x1, Pallas kernels: none -> 2.69 us  [pack(): pl.pallas_call(pack_kernel, out_shape=jax.ShapeDtypeStruct((tiles, 1, (le...]
    mul x2 -> x0, other arithmetic: 1.81 us -> none  [pack_soundings(): snd_kernel * root[:, :, None, :]]
    convert_element_type x2 -> x0, other arithmetic: 1.51 us -> none  [the longest x1 0.79 us: pack_soundings(): snd_column.astype(jnp.float32)]
    concatenate x1 -> x0, other arithmetic: 0.99 us -> none  [pack_soundings(): jnp.concatenate([p.reshape(tile_count, 1, -1) for p in parts], axis=2)]
where the time goes in v3:
time: 91.7 us; the launch traced here: 91.2 us
  starting transfers between devices  38.4 us (42%)
  waiting for transfers between devices  29.6 us (32%)
  Pallas kernels  23.2 us (25%)
    ppermute x5, waiting for transfers between devices, shifted(): lax.ppermute(block, RING, [(i, (i + distance) % total) for i in range(tot...  29.5 us
    ppermute x5, starting transfers between devices, shifted(): lax.ppermute(block, RING, [(i, (i + distance) % total) for i in range(tot...  20.4 us
    all_to_all x1, starting transfers between devices, program(): lax.all_to_all(packed, 'tile', split_axis=0, concat_axis=0, tiled=True)  18 us
    pallas_call x1, Pallas kernels, adjoint_to_edges(): pl.pallas_call(sounding_kernel, out_shape=shapes_of(adjoint_in, adjoint_i...  11.4 us
    pallas_call x1, Pallas kernels, forward(): pl.pallas_call(forward_kernel, out_shape=jax.ShapeDtypeStruct((2 * SLOT_R...  4.09 us
    pallas_call x1, Pallas kernels, adjoint_final(): pl.pallas_call(final_kernel, out_shape=jax.ShapeDtypeStruct(shape, jnp.fl...  2.94 us
    pallas_call x1, Pallas kernels, pack(): pl.pallas_call(pack_kernel, out_shape=jax.ShapeDtypeStruct((tiles, 1, (le...  2.69 us
    pallas_call x1, Pallas kernels, rims(): pl.pallas_call(rim_kernel, out_shape=edges + shapes_of(*winds), in_specs=...  2.09 us
  transfers between devices with their start and end apart: 6, of which 4 were waited for; matrix products, arithmetic and copies ran while one was open for 0% of the time, Pallas kernels for 7%

profile of v3, /device:TPU:24, one launch (start us, length us, event | category | flops | bytes accessed | tf_op | source)
XLA Modules:
  0.0 91.2 jit_solution(10421716338540187116)
XLA Ops:
  0.0 2.7 %shard_map.111 = f32[32,1,2432]{2,1,0:T(1,128)} custom-call(s32[1,32]{1,0:T(1,128)} %count.1, s32[1,32,128]{2,1,0:T(8,128)} %refs_0_.3, s32[1,32,128]{2,1,0:T(8,128)} %refs_1_.3, f32[1,32,128]{2,1,0:T(8,128)} %refs_2_.3, f32[1,32,128]{2,1,0:T(8,128)} %refs_3_.1, f32[1,32,16,128]{3,2,1,0:T(8,128)} %refs_4_.1), custom_call_target="tpu_custom_call" | custom-call | tf_op jit(solution)/shard_map/pallas_call | solution.py:303
  2.7 18.0 %all-to-all-start = ((f32[32,1,2432]{2,1,0:T(1,128)}), f32[32,1,2432]{2,1,0:T(1,128)S(1)}, u32[]{:S(2)}, u32[]{:S(2)}) async-start(f32[32,1,2432]{2,1,0:T(1,128)} %shard_map.111), calls=%async_computation | async-start | bytes 622592 | tf_op jit(solution)/shard_map/all_to_all | solution.py:460
  20.7 1.9 %collective-permute-start = (f32[16,16,768]{2,1,0:T(8,128)}, f32[16,16,768]{2,1,0:T(8,128)S(1)}, u32[]{:S(2)}, u32[]{:S(2)}) collective-permute-start(f32[16,16,768]{2,1,0:T(8,128)} %param.11), channel_id=1, source_target_pairs={{0,32},{1,33},{2,34},{3,35},{4,36},{5,37},{6,38},{7,39},{8,40},{9,... | collective-permute-start | bytes 2359304 | tf_op jit(solution)/shard_map/ppermute | solution.py:16
  22.6 14.7 %collective-permute-done.refs_3_.tracer = f32[16,16,768]{2,1,0:T(8,128)S(1)} collective-permute-done((f32[16,16,768]{2,1,0:T(8,128)}, f32[16,16,768]{2,1,0:T(8,128)S(1)}, u32[]{:S(2)}, u32[]{:S(2)}) %collective-permute-start) | collective-permute-done | bytes 786464 | tf_op jit(solution)/shard_map/ppermute | solution.py:16
  37.3 2.1 %shard_map.109 = (f32[7,16,768]{2,1,0:T(8,128)S(1)}, f32[5,16,768]{2,1,0:T(8,128)S(1)}, f32[16,16,768]{2,1,0:T(8,128)S(1)}, f32[16,16,768]{2,1,0:T(8,128)S(1)}, f32[15,16,768]{2,1,0:T(8,128)S(1)}) custom-call(f32[16,16,768]{2,1,0:T(8,128)} %far_courant_x.1, f32[16,16,768]{2,1,0:T(8,128)} %far_courant_y.1, f32[15,16,768]{2,1,0:T(8,128)} %far_mixing.1, ...), custom_call_target="tpu_custom_call" | custom-call | tf_op jit(solution)/shard_map/pallas_call | solution.py:360
  39.4 3.6 %collective-permute-start.1 = (f32[7,16,768]{2,1,0:T(8,128)S(1)}, f32[7,16,768]{2,1,0:T(8,128)S(1)}, u32[]{:S(2)}, u32[]{:S(2)}) collective-permute-start(f32[7,16,768]{2,1,0:T(8,128)S(1)} %get-tuple-element.17), channel_id=1, source_target_pairs={{0,1},{1,2},{2,3},{3,4},{4,5},{5,6},{6,7},{7,8},{8,9},{9,10},{10,1... | collective-permute-start | bytes 1032200 | tf_op jit(solution)/shard_map/ppermute | solution.py:16
  43.0 6.2 %collective-permute-start.2 = (f32[5,16,768]{2,1,0:T(8,128)S(1)}, f32[5,16,768]{2,1,0:T(8,128)S(1)}, u32[]{:S(2)}, u32[]{:S(2)}) collective-permute-start(f32[5,16,768]{2,1,0:T(8,128)S(1)} %get-tuple-element.18), channel_id=1, source_target_pairs={{0,511},{1,0},{2,1},{3,2},{4,3},{5,4},{6,5},{7,6},{8,7},{9,8},{10,... | collective-permute-start | bytes 737288 | tf_op jit(solution)/shard_map/ppermute | solution.py:16
  49.2 5.1 %collective-permute-done.2.high.rim_high = f32[5,16,768]{2,1,0:T(8,128)S(1)} collective-permute-done((f32[5,16,768]{2,1,0:T(8,128)S(1)}, f32[5,16,768]{2,1,0:T(8,128)S(1)}, u32[]{:S(2)}, u32[]{:S(2)}) %collective-permute-start.2) | collective-permute-done | bytes 245792 | tf_op jit(solution)/shard_map/ppermute | solution.py:16
  54.4 1.4 %collective-permute-done.1.low.rim_low = f32[7,16,768]{2,1,0:T(8,128)S(1)} collective-permute-done((f32[7,16,768]{2,1,0:T(8,128)S(1)}, f32[7,16,768]{2,1,0:T(8,128)S(1)}, u32[]{:S(2)}, u32[]{:S(2)}) %collective-permute-start.1) | collective-permute-done | bytes 344096 | tf_op jit(solution)/shard_map/ppermute | solution.py:16
  55.8 4.1 %shard_map.110.table = f32[3072,128]{1,0:T(8,128)S(1)} custom-call(f32[16,16,768]{2,1,0:T(8,128)S(1)} %collective-permute-done.refs_3_.tracer, f32[7,16,768]{2,1,0:T(8,128)S(1)} %collective-permute-done.1.low.rim_low, f32[5,16,768]{2,1,0:T(8,128)S(1)} %collective-permute-done.2.high.rim_high, f32[16,16,768]{2,1,0:T(8,128)S(1)} %get-tuple-element.19.courant_x, ...), custom_call_target="tpu_custom_call" | custom-call | tf_op jit(solution)/shard_map/pallas_call | solution.py:429
  59.9 0.0 all-to-all-done.box
  59.9 11.4 %shard_map.112 = (f32[16,16,768]{2,1,0:T(8,128)S(1)}, f32[16,16,768]{2,1,0:T(8,128)S(1)}, f32[4,16,768]{2,1,0:T(8,128)S(1)}, f32[2,16,768]{2,1,0:T(8,128)S(1)}, ...) custom-call(f32[3072,128]{1,0:T(8,128)S(1)} %shard_map.110.table, ...), custom_call_target="tpu_custom_call" | custom-call | tf_op jit(solution)/shard_map/pallas_call | solution.py:181
  71.3 6.8 %collective-permute-start.4 = (f32[4,16,768]{2,1,0:T(8,128)S(1)}, f32[4,16,768]{2,1,0:T(8,128)S(1)}, u32[]{:S(2)}, u32[]{:S(2)}) collective-permute-start(f32[4,16,768]{2,1,0:T(8,128)S(1)} %get-tuple-element.28), channel_id=1, source_target_pairs={{0,511},{1,0},{2,1},{3,2},{4,3},{5,4},{6,5},{7,6},{8,7},{9,8},{10,... | collective-permute-start | bytes 589832 | tf_op jit(solution)/shard_map/ppermute | solution.py:16
  78.1 1.9 %collective-permute-start.3 = (f32[2,16,768]{2,1,0:T(8,128)S(1)}, f32[2,16,768]{2,1,0:T(8,128)S(1)}, u32[]{:S(2)}, u32[]{:S(2)}) collective-permute-start(f32[2,16,768]{2,1,0:T(8,128)S(1)} %get-tuple-element.27), channel_id=1, source_target_pairs={{0,1},{1,2},{2,3},{3,4},{4,5},{5,6},{6,7},{7,8},{8,9},{9,10},{10,1... | collective-permute-start | bytes 294920 | tf_op jit(solution)/shard_map/ppermute | solution.py:16
  80.0 8.2 %collective-permute-done.3.low = f32[2,16,768]{2,1,0:T(8,128)S(1)} collective-permute-done((f32[2,16,768]{2,1,0:T(8,128)S(1)}, f32[2,16,768]{2,1,0:T(8,128)S(1)}, u32[]{:S(2)}, u32[]{:S(2)}) %collective-permute-start.3) | collective-permute-done | bytes 98336 | tf_op jit(solution)/shard_map/ppermute | solution.py:16
  88.2 0.0 collective-permute-done.4.high
  88.2 2.9 %shard_map.113 = f32[16,16,768]{2,1,0:T(8,128)} custom-call(f32[16,16,768]{2,1,0:T(8,128)S(1)} %get-tuple-element.22.swept_1, f32[16,16,768]{2,1,0:T(8,128)S(1)} %get-tuple-element.23.forcing_0, f32[16,16,768]{2,1,0:T(8,128)S(1)} %get-tuple-element.24.courant_x, f32[16,16,768]{2,1,0:T(8,128)S(1)} %get-tuple-element.25.courant_y, ...), custom_call_target="tpu_custom_call" | custom-call | tf_op jit(solution)/shard_map/pallas_call | solution.py:254
Async XLA Ops:
  2.7 57.2 %all-to-all-start = ((f32[32,1,2432]{2,1,0:T(1,128)}), f32[32,1,2432]{2,1,0:T(1,128)S(1)}, u32[]{:S(2)}, u32[]{:S(2)}) async-start(f32[32,1,2432]{2,1,0:T(1,128)} %shard_map.111), calls=%async_computation | async-start | bytes 622592 | tf_op jit(solution)/shard_map/all_to_all | solution.py:460
  20.7 16.7 %collective-permute-start = (f32[16,16,768]{2,1,0:T(8,128)}, f32[16,16,768]{2,1,0:T(8,128)S(1)}, u32[]{:S(2)}, u32[]{:S(2)}) collective-permute-start(f32[16,16,768]{2,1,0:T(8,128)} %param.11), channel_id=1, source_target_pairs={{0,32},{1,33},{2,34},{3,35},{4,36},{5,37},{6,38},{7,39},{8,40},{9,... | collective-permute-start | bytes 2359304 | tf_op jit(solution)/shard_map/ppermute | solution.py:16
  39.4 16.4 %collective-permute-start.1 = (f32[7,16,768]{2,1,0:T(8,128)S(1)}, f32[7,16,768]{2,1,0:T(8,128)S(1)}, u32[]{:S(2)}, u32[]{:S(2)}) collective-permute-start(f32[7,16,768]{2,1,0:T(8,128)S(1)} %get-tuple-element.17), channel_id=1, source_target_pairs={{0,1},{1,2},{2,3},{3,4},{4,5},{5,6},{6,7},{7,8},{8,9},{9,10},{10,1... | collective-permute-start | bytes 1032200 | tf_op jit(solution)/shard_map/ppermute | solution.py:16
  43.0 11.4 %collective-permute-start.2 = (f32[5,16,768]{2,1,0:T(8,128)S(1)}, f32[5,16,768]{2,1,0:T(8,128)S(1)}, u32[]{:S(2)}, u32[]{:S(2)}) collective-permute-start(f32[5,16,768]{2,1,0:T(8,128)S(1)} %get-tuple-element.18), channel_id=1, source_target_pairs={{0,511},{1,0},{2,1},{3,2},{4,3},{5,4},{6,5},{7,6},{8,7},{9,8},{10,... | collective-permute-start | bytes 737288 | tf_op jit(solution)/shard_map/ppermute | solution.py:16
  71.3 16.9 %collective-permute-start.4 = (f32[4,16,768]{2,1,0:T(8,128)S(1)}, f32[4,16,768]{2,1,0:T(8,128)S(1)}, u32[]{:S(2)}, u32[]{:S(2)}) collective-permute-start(f32[4,16,768]{2,1,0:T(8,128)S(1)} %get-tuple-element.28), channel_id=1, source_target_pairs={{0,511},{1,0},{2,1},{3,2},{4,3},{5,4},{6,5},{7,6},{8,7},{9,8},{10,... | collective-permute-start | bytes 589832 | tf_op jit(solution)/shard_map/ppermute | solution.py:16
  78.1 10.2 %collective-permute-start.3 = (f32[2,16,768]{2,1,0:T(8,128)S(1)}, f32[2,16,768]{2,1,0:T(8,128)S(1)}, u32[]{:S(2)}, u32[]{:S(2)}) collective-permute-start(f32[2,16,768]{2,1,0:T(8,128)S(1)} %get-tuple-element.27), channel_id=1, source_target_pairs={{0,1},{1,2},{2,3},{3,4},{4,5},{5,6},{6,7},{7,8},{8,9},{9,10},{10,1... | collective-permute-start | bytes 294920 | tf_op jit(solution)/shard_map/ppermute | solution.py:16

commit v4 on v3

--- a/solution.py
+++ b/solution.py
@@ -48,7 +48,7 @@
     far_courant_y,
     far_mixing,
     forcing_0,
-    swept_1,
+    forcing_1,
     to_low,
     to_high,
     courant_x,
@@ -56,7 +56,6 @@
     mixing,
     adjoint_in,
     field_done,
-    forcing_1,
     row_wide,
     row_ref,
     row_done,
@@ -148,9 +147,45 @@
         return carry
 
     lax.fori_loop(0, 6, back, 0)
-    levels = adjoint_in.shape[0]
     for copy in copies:
         copy.wait()
+    b = {}
+    for x in (0, 1, 2, 3, 14, 15):
+        entering = adjoint_in[:, x, :] + forcing_1[:, x, :]
+        b[x] = sweep_y(mix_rows(entering, mixing_row(mixing, x)), courant_y[:, x, :])
+    g = {x: courant_x[:, x, :] * (b[x + 1] - b[x]) for x in (0, 1, 2, 14)}
+    to_low[0] = b[0]
+    to_low[1] = g[0]
+    to_low[2] = b[0] + (5.0 * g[0] - g[1]) * (1.0 / 6.0) + forcing_0[:, 0, :]
+    a = b[1] + (2.0 * g[0] + 5.0 * g[1] - g[2]) * (1.0 / 6.0) + forcing_0[:, 1, :]
+    to_low[3] = sweep_y(mix_rows(a, mixing_row(mixing, 1)), courant_y[:, 1, :])
+    to_high[0] = b[15]
+    to_high[1] = b[15] + g[14] * (1.0 / 3.0) + forcing_0[:, 15, :]
+
+
+def adjoint_to_edges(table, box, adjoint_in, *winds):
+    vmem, hbm = (pl.BlockSpec(memory_space=space) for space in (pltpu.VMEM, pltpu.HBM))
+    levels, _, width_y = adjoint_in.shape
+    edges = tuple(jax.ShapeDtypeStruct((n, levels, width_y), jnp.float32) for n in (4, 2))
+    return pl.pallas_call(
+        sounding_kernel,
+        out_shape=shapes_of(adjoint_in, adjoint_in) + edges + shapes_of(*winds, adjoint_in),
+        in_specs=[vmem] * 2 + [hbm] * 4,
+        out_specs=(vmem,) * 8,
+        scratch_shapes=[
+            pltpu.SemaphoreType.DMA((4,)),
+            pltpu.VMEM((box.shape[0], 128), jnp.int32),
+            pltpu.SMEM((box.shape[0], 128), jnp.int32),
+            pltpu.SemaphoreType.DMA,
+        ]
+        + [pltpu.VMEM((128, 128), jnp.float32)] * 4
+        + [pltpu.VMEM((2 * SLOT_ROWS, 128), jnp.float32)] * 8,
+        compiler_params=pltpu.CompilerParams(vmem_limit_bytes=26 * 2**20),
+    )(table, box, adjoint_in, *winds)
+
+
+def inner_kernel(adjoint_in, forcing_1, courant_y, mixing, swept_1):
+    levels = adjoint_in.shape[0]
 
     def first_step(level, carry):
         here, below = carry
@@ -163,38 +198,17 @@
 
     start = adjoint_in[0] + forcing_1[0]
     lax.fori_loop(0, levels, first_step, (start, jnp.zeros_like(start)), unroll=UNROLL)
-    b = {x: swept_1[:, x, :] for x in (0, 1, 2, 3, 14, 15)}
-    g = {x: courant_x[:, x, :] * (b[x + 1] - b[x]) for x in (0, 1, 2, 14)}
-    to_low[0] = b[0]
-    to_low[1] = g[0]
-    to_low[2] = b[0] + (5.0 * g[0] - g[1]) * (1.0 / 6.0) + forcing_0[:, 0, :]
-    a = b[1] + (2.0 * g[0] + 5.0 * g[1] - g[2]) * (1.0 / 6.0) + forcing_0[:, 1, :]
-    to_low[3] = sweep_y(mix_rows(a, mixing_row(mixing, 1)), courant_y[:, 1, :])
-    to_high[0] = b[15]
-    to_high[1] = b[15] + g[14] * (1.0 / 3.0) + forcing_0[:, 15, :]
-
-
-def adjoint_to_edges(table, box, adjoint_in, *winds):
-    vmem, hbm = (pl.BlockSpec(memory_space=space) for space in (pltpu.VMEM, pltpu.HBM))
-    levels, _, width_y = adjoint_in.shape
-    edges = tuple(jax.ShapeDtypeStruct((n, levels, width_y), jnp.float32) for n in (4, 2))
+
+
+def adjoint_inner(*fields):
+    vmem = pl.BlockSpec(memory_space=pltpu.VMEM)
     return pl.pallas_call(
-        sounding_kernel,
-        out_shape=shapes_of(adjoint_in, adjoint_in) + edges + shapes_of(*winds),
-        in_specs=[vmem] * 2 + [hbm] * 4,
-        out_specs=(vmem,) * 7,
-        scratch_shapes=[
-            pltpu.VMEM(adjoint_in.shape, jnp.float32),
-            pltpu.SemaphoreType.DMA((4,)),
-            pltpu.VMEM(adjoint_in.shape, jnp.float32),
-            pltpu.VMEM((box.shape[0], 128), jnp.int32),
-            pltpu.SMEM((box.shape[0], 128), jnp.int32),
-            pltpu.SemaphoreType.DMA,
-        ]
-        + [pltpu.VMEM((128, 128), jnp.float32)] * 4
-        + [pltpu.VMEM((2 * SLOT_ROWS, 128), jnp.float32)] * 8,
-        compiler_params=pltpu.CompilerParams(vmem_limit_bytes=26 * 2**20),
-    )(table, box, adjoint_in, *winds)
+        inner_kernel,
+        out_shape=jax.ShapeDtypeStruct(fields[0].shape, jnp.float32),
+        in_specs=[vmem] * len(fields),
+        out_specs=vmem,
+        compiler_params=pltpu.CompilerParams(vmem_limit_bytes=4 * 2**20),
+    )(*fields)
 
 
 def final_kernel(
@@ -462,11 +476,12 @@
     low = shifted(to_high, 1)
     high = shifted(to_low, -1)
     table = forward(tracer, low, high, *near_winds)
-    forcing_0, swept_1, to_low, to_high, *near_winds = adjoint_to_edges(
+    forcing_0, forcing_1, to_low, to_high, *near_winds, near_adjoint = adjoint_to_edges(
         table, box, adjoint_in, *winds
     )
     from_high = shifted(to_low, -1)
     from_low = shifted(to_high, 1)
+    swept_1 = adjoint_inner(near_adjoint, forcing_1, *near_winds[1:])
     return adjoint_final(
         swept_1, forcing_0, *near_winds, from_low, from_high, low, high
     )

time: 91.7 us -> 91 us (level)
  waiting for transfers between devices: 29.6 us -> 28.3 us
    ppermute x5, waiting for transfers between devices: 29.5 us -> 28.3 us  [shifted(): lax.ppermute(block, RING, [(i, (i + distance) % total) for i in range(tot...]
    pallas_call x0 -> x1, Pallas kernels: none -> 1.26 us  [adjoint_inner(): pl.pallas_call(inner_kernel, out_shape=jax.ShapeDtypeStruct(fields[0].sha...]
  transfers between devices with their start and end apart: 6 -> 6, of which waited for: 4 -> 4; matrix products, arithmetic and copies ran while one was open for 0% -> 0% of each run, Pallas kernels for 7% -> 8%
where the time goes in v4:
time: 91 us; the launch traced here: 90.4 us
  starting transfers between devices  38.4 us (42%)
  waiting for transfers between devices  28.3 us (31%)
  Pallas kernels  23.7 us (26%)
    ppermute x5, waiting for transfers between devices, shifted(): lax.ppermute(block, RING, [(i, (i + distance) % total) for i in range(tot...  28.3 us
    ppermute x5, starting transfers between devices, shifted(): lax.ppermute(block, RING, [(i, (i + distance) % total) for i in range(tot...  20.4 us
    all_to_all x1, starting transfers between devices, program(): lax.all_to_all(packed, 'tile', split_axis=0, concat_axis=0, tiled=True)  18 us
    pallas_call x1, Pallas kernels, adjoint_to_edges(): pl.pallas_call(sounding_kernel, out_shape=shapes_of(adjoint_in, adjoint_i...  10.6 us
    pallas_call x1, Pallas kernels, forward(): pl.pallas_call(forward_kernel, out_shape=jax.ShapeDtypeStruct((2 * SLOT_R...  4.09 us
    pallas_call x1, Pallas kernels, adjoint_final(): pl.pallas_call(final_kernel, out_shape=jax.ShapeDtypeStruct(shape, jnp.fl...  2.94 us
    pallas_call x1, Pallas kernels, pack(): pl.pallas_call(pack_kernel, out_shape=jax.ShapeDtypeStruct((tiles, 1, (le...  2.69 us
    pallas_call x1, Pallas kernels, rims(): pl.pallas_call(rim_kernel, out_shape=edges + shapes_of(*winds), in_specs=...  2.09 us
  transfers between devices with their start and end apart: 6, of which 4 were waited for; matrix products, arithmetic and copies ran while one was open for 0% of the time, Pallas kernels for 8%

profile of v4, /device:TPU:24, one launch (start us, length us, event | category | flops | bytes accessed | tf_op | source)
XLA Modules:
  0.0 90.4 jit_solution(17906192785028344716)
XLA Ops:
  0.0 2.7 %shard_map.111 = f32[32,1,2432]{2,1,0:T(1,128)} custom-call(s32[1,32]{1,0:T(1,128)} %count.1, s32[1,32,128]{2,1,0:T(8,128)} %refs_0_.3, s32[1,32,128]{2,1,0:T(8,128)} %refs_1_.3, f32[1,32,128]{2,1,0:T(8,128)} %refs_2_.3, f32[1,32,128]{2,1,0:T(8,128)} %refs_3_.1, f32[1,32,16,128]{3,2,1,0:T(8,128)} %refs_4_.1), custom_call_target="tpu_custom_call" | custom-call | tf_op jit(solution)/shard_map/pallas_call | solution.py:317
  2.7 18.0 %all-to-all-start = ((f32[32,1,2432]{2,1,0:T(1,128)}), f32[32,1,2432]{2,1,0:T(1,128)S(1)}, u32[]{:S(2)}, u32[]{:S(2)}) async-start(f32[32,1,2432]{2,1,0:T(1,128)} %shard_map.111), calls=%async_computation | async-start | bytes 622592 | tf_op jit(solution)/shard_map/all_to_all | solution.py:474
  20.7 1.9 %collective-permute-start = (f32[16,16,768]{2,1,0:T(8,128)}, f32[16,16,768]{2,1,0:T(8,128)S(1)}, u32[]{:S(2)}, u32[]{:S(2)}) collective-permute-start(f32[16,16,768]{2,1,0:T(8,128)} %param.11), channel_id=1, source_target_pairs={{0,32},{1,33},{2,34},{3,35},{4,36},{5,37},{6,38},{7,39},{8,40},{9,... | collective-permute-start | bytes 2359304 | tf_op jit(solution)/shard_map/ppermute | solution.py:16
  22.6 14.7 %collective-permute-done.refs_3_.tracer = f32[16,16,768]{2,1,0:T(8,128)S(1)} collective-permute-done((f32[16,16,768]{2,1,0:T(8,128)}, f32[16,16,768]{2,1,0:T(8,128)S(1)}, u32[]{:S(2)}, u32[]{:S(2)}) %collective-permute-start) | collective-permute-done | bytes 786464 | tf_op jit(solution)/shard_map/ppermute | solution.py:16
  37.3 2.1 %shard_map.109 = (f32[7,16,768]{2,1,0:T(8,128)S(1)}, f32[5,16,768]{2,1,0:T(8,128)S(1)}, f32[16,16,768]{2,1,0:T(8,128)S(1)}, f32[16,16,768]{2,1,0:T(8,128)S(1)}, f32[15,16,768]{2,1,0:T(8,128)S(1)}) custom-call(f32[16,16,768]{2,1,0:T(8,128)} %far_courant_x.1, f32[16,16,768]{2,1,0:T(8,128)} %far_courant_y.1, f32[15,16,768]{2,1,0:T(8,128)} %far_mixing.1, ...), custom_call_target="tpu_custom_call" | custom-call | tf_op jit(solution)/shard_map/pallas_call | solution.py:374
  39.4 3.6 %collective-permute-start.1 = (f32[7,16,768]{2,1,0:T(8,128)S(1)}, f32[7,16,768]{2,1,0:T(8,128)S(1)}, u32[]{:S(2)}, u32[]{:S(2)}) collective-permute-start(f32[7,16,768]{2,1,0:T(8,128)S(1)} %get-tuple-element.18), channel_id=1, source_target_pairs={{0,1},{1,2},{2,3},{3,4},{4,5},{5,6},{6,7},{7,8},{8,9},{9,10},{10,1... | collective-permute-start | bytes 1032200 | tf_op jit(solution)/shard_map/ppermute | solution.py:16
  43.0 6.2 %collective-permute-start.2 = (f32[5,16,768]{2,1,0:T(8,128)S(1)}, f32[5,16,768]{2,1,0:T(8,128)S(1)}, u32[]{:S(2)}, u32[]{:S(2)}) collective-permute-start(f32[5,16,768]{2,1,0:T(8,128)S(1)} %get-tuple-element.19), channel_id=1, source_target_pairs={{0,511},{1,0},{2,1},{3,2},{4,3},{5,4},{6,5},{7,6},{8,7},{9,8},{10,... | collective-permute-start | bytes 737288 | tf_op jit(solution)/shard_map/ppermute | solution.py:16
  49.2 5.1 %collective-permute-done.2.high.rim_high = f32[5,16,768]{2,1,0:T(8,128)S(1)} collective-permute-done((f32[5,16,768]{2,1,0:T(8,128)S(1)}, f32[5,16,768]{2,1,0:T(8,128)S(1)}, u32[]{:S(2)}, u32[]{:S(2)}) %collective-permute-start.2) | collective-permute-done | bytes 245792 | tf_op jit(solution)/shard_map/ppermute | solution.py:16
  54.4 1.4 %collective-permute-done.1.low.rim_low = f32[7,16,768]{2,1,0:T(8,128)S(1)} collective-permute-done((f32[7,16,768]{2,1,0:T(8,128)S(1)}, f32[7,16,768]{2,1,0:T(8,128)S(1)}, u32[]{:S(2)}, u32[]{:S(2)}) %collective-permute-start.1) | collective-permute-done | bytes 344096 | tf_op jit(solution)/shard_map/ppermute | solution.py:16
  55.8 4.1 %shard_map.110.table = f32[3072,128]{1,0:T(8,128)S(1)} custom-call(f32[16,16,768]{2,1,0:T(8,128)S(1)} %collective-permute-done.refs_3_.tracer, f32[7,16,768]{2,1,0:T(8,128)S(1)} %collective-permute-done.1.low.rim_low, f32[5,16,768]{2,1,0:T(8,128)S(1)} %collective-permute-done.2.high.rim_high, f32[16,16,768]{2,1,0:T(8,128)S(1)} %get-tuple-element.20.courant_x, ...), custom_call_target="tpu_custom_call" | custom-call | tf_op jit(solution)/shard_map/pallas_call | solution.py:443
  59.9 0.0 all-to-all-done.box
  59.9 10.6 %shard_map.112 = (f32[16,16,768]{2,1,0:T(8,128)S(1)}, f32[16,16,768]{2,1,0:T(8,128)S(1)}, f32[4,16,768]{2,1,0:T(8,128)S(1)}, f32[2,16,768]{2,1,0:T(8,128)S(1)}, ...) custom-call(f32[3072,128]{1,0:T(8,128)S(1)} %shard_map.110.table, ...), custom_call_target="tpu_custom_call" | custom-call | tf_op jit(solution)/shard_map/pallas_call | solution.py:170
  70.5 6.8 %collective-permute-start.4 = (f32[4,16,768]{2,1,0:T(8,128)S(1)}, f32[4,16,768]{2,1,0:T(8,128)S(1)}, u32[]{:S(2)}, u32[]{:S(2)}) collective-permute-start(f32[4,16,768]{2,1,0:T(8,128)S(1)} %get-tuple-element.30), channel_id=1, source_target_pairs={{0,511},{1,0},{2,1},{3,2},{4,3},{5,4},{6,5},{7,6},{8,7},{9,8},{10,... | collective-permute-start | bytes 589832 | tf_op jit(solution)/shard_map/ppermute | solution.py:16
  77.3 1.9 %collective-permute-start.3 = (f32[2,16,768]{2,1,0:T(8,128)S(1)}, f32[2,16,768]{2,1,0:T(8,128)S(1)}, u32[]{:S(2)}, u32[]{:S(2)}) collective-permute-start(f32[2,16,768]{2,1,0:T(8,128)S(1)} %get-tuple-element.29), channel_id=1, source_target_pairs={{0,1},{1,2},{2,3},{3,4},{4,5},{5,6},{6,7},{7,8},{8,9},{9,10},{10,1... | collective-permute-start | bytes 294920 | tf_op jit(solution)/shard_map/ppermute | solution.py:16
  79.3 1.3 %shard_map.113.swept_1 = f32[16,16,768]{2,1,0:T(8,128)S(1)} custom-call(f32[16,16,768]{2,1,0:T(8,128)S(1)} %get-tuple-element.23.adjoint_in, f32[16,16,768]{2,1,0:T(8,128)S(1)} %get-tuple-element.24.forcing_1, f32[16,16,768]{2,1,0:T(8,128)S(1)} %get-tuple-element.25.courant_y, f32[15,16,768]{2,1,0:T(8,128)S(1)} %get-tuple-element.26.mixing), custom_call_target="tpu_custom_call" | custom-call | tf_op jit(solution)/shard_map/pallas_call | solution.py:205
  80.5 7.0 %collective-permute-done.3.low = f32[2,16,768]{2,1,0:T(8,128)S(1)} collective-permute-done((f32[2,16,768]{2,1,0:T(8,128)S(1)}, f32[2,16,768]{2,1,0:T(8,128)S(1)}, u32[]{:S(2)}, u32[]{:S(2)}) %collective-permute-start.3) | collective-permute-done | bytes 98336 | tf_op jit(solution)/shard_map/ppermute | solution.py:16
  87.5 0.0 collective-permute-done.4.high
  87.5 2.9 %shard_map.114 = f32[16,16,768]{2,1,0:T(8,128)} custom-call(f32[16,16,768]{2,1,0:T(8,128)S(1)} %shard_map.113.swept_1, f32[16,16,768]{2,1,0:T(8,128)S(1)} %get-tuple-element.27.forcing_0, f32[16,16,768]{2,1,0:T(8,128)S(1)} %get-tuple-element.28.courant_x, f32[16,16,768]{2,1,0:T(8,128)S(1)} %get-tuple-element.25.courant_y, ...), custom_call_target="tpu_custom_call" | custom-call | tf_op jit(solution)/shard_map/pallas_call | solution.py:268
Async XLA Ops:
  2.7 57.2 %all-to-all-start = ((f32[32,1,2432]{2,1,0:T(1,128)}), f32[32,1,2432]{2,1,0:T(1,128)S(1)}, u32[]{:S(2)}, u32[]{:S(2)}) async-start(f32[32,1,2432]{2,1,0:T(1,128)} %shard_map.111), calls=%async_computation | async-start | bytes 622592 | tf_op jit(solution)/shard_map/all_to_all | solution.py:474
  20.7 16.7 %collective-permute-start = (f32[16,16,768]{2,1,0:T(8,128)}, f32[16,16,768]{2,1,0:T(8,128)S(1)}, u32[]{:S(2)}, u32[]{:S(2)}) collective-permute-start(f32[16,16,768]{2,1,0:T(8,128)} %param.11), channel_id=1, source_target_pairs={{0,32},{1,33},{2,34},{3,35},{4,36},{5,37},{6,38},{7,39},{8,40},{9,... | collective-permute-start | bytes 2359304 | tf_op jit(solution)/shard_map/ppermute | solution.py:16
  39.4 16.4 %collective-permute-start.1 = (f32[7,16,768]{2,1,0:T(8,128)S(1)}, f32[7,16,768]{2,1,0:T(8,128)S(1)}, u32[]{:S(2)}, u32[]{:S(2)}) collective-permute-start(f32[7,16,768]{2,1,0:T(8,128)S(1)} %get-tuple-element.18), channel_id=1, source_target_pairs={{0,1},{1,2},{2,3},{3,4},{4,5},{5,6},{6,7},{7,8},{8,9},{9,10},{10,1... | collective-permute-start | bytes 1032200 | tf_op jit(solution)/shard_map/ppermute | solution.py:16
  43.0 11.4 %collective-permute-start.2 = (f32[5,16,768]{2,1,0:T(8,128)S(1)}, f32[5,16,768]{2,1,0:T(8,128)S(1)}, u32[]{:S(2)}, u32[]{:S(2)}) collective-permute-start(f32[5,16,768]{2,1,0:T(8,128)S(1)} %get-tuple-element.19), channel_id=1, source_target_pairs={{0,511},{1,0},{2,1},{3,2},{4,3},{5,4},{6,5},{7,6},{8,7},{9,8},{10,... | collective-permute-start | bytes 737288 | tf_op jit(solution)/shard_map/ppermute | solution.py:16
  70.5 16.9 %collective-permute-start.4 = (f32[4,16,768]{2,1,0:T(8,128)S(1)}, f32[4,16,768]{2,1,0:T(8,128)S(1)}, u32[]{:S(2)}, u32[]{:S(2)}) collective-permute-start(f32[4,16,768]{2,1,0:T(8,128)S(1)} %get-tuple-element.30), channel_id=1, source_target_pairs={{0,511},{1,0},{2,1},{3,2},{4,3},{5,4},{6,5},{7,6},{8,7},{9,8},{10,... | collective-permute-start | bytes 589832 | tf_op jit(solution)/shard_map/ppermute | solution.py:16
  77.3 10.2 %collective-permute-start.3 = (f32[2,16,768]{2,1,0:T(8,128)S(1)}, f32[2,16,768]{2,1,0:T(8,128)S(1)}, u32[]{:S(2)}, u32[]{:S(2)}) collective-permute-start(f32[2,16,768]{2,1,0:T(8,128)S(1)} %get-tuple-element.29), channel_id=1, source_target_pairs={{0,1},{1,2},{2,3},{3,4},{4,5},{5,6},{6,7},{7,8},{8,9},{9,10},{10,1... | collective-permute-start | bytes 294920 | tf_op jit(solution)/shard_map/ppermute | solution.py:16
